TPU v7x, 32 devices: a whole 2x2x4 slice. The times are simulated.
32 devices in a mesh: tm: 2 (over x), space: 16 (over z, y, core).
Axes of the slice: x: 2, y: 2, z: 4, core: 2. Of those that a mesh axis runs over, the one named last changes fastest.
Arguments:
- slice_ends: float32 [8, 2, 64, 16, 256], P('tm', None, 'space'), may hold values from 0.05 to 0.6
- initial: float32 [2, 64, 16, 256], P(None, 'space'), may hold values from 0.05 to 0.6
- feed_rate: float32 [64, 16, 256], P('space'), may hold values from 0.02 to 0.12
- kill_rate: float32 [64, 16, 256], P('space'), may hold values from 0.03 to 0.12
Outputs:
- new_ends: float32 [8, 2, 64, 16, 256], P('tm', None, 'space')
All inputs are finite; a program needn't handle non-finite values.
Results may differ from a plain program's by a relative error of at most 0.0001.
Values sent between devices are 32-bit elements; how exact they have to be, the bound alone decides.
No kernel may reach another device: no remote copies, remote signals or barrier semaphores. Data moves between devices by JAX's collectives and lax.ppermute only.
A program may use at most 64 MiB of HBM per device.

v0:
```python
import jax
import jax.numpy as jnp
from jax import lax
from jax.sharding import PartitionSpec as P

NF = 8
KC = 8


spread_fast = 0.14
spread_slow = 0.07
fine_step = 0.25
coarse_step = 1.0


def padded(value, sides, width):
    for axis, dim in sides:
        size, length = (lax.axis_size(axis), value.shape[dim])
        up = [(i, (i + 1) % size) for i in range(size)]
        down = [(j, i) for i, j in up]
        last = lax.slice_in_dim(value, length - width, length, axis=dim)
        initial = lax.slice_in_dim(value, 0, width, axis=dim)
        before = lax.ppermute(last, axis, up)
        after = lax.ppermute(initial, axis, down)
        value = jnp.concatenate([before, value, after], axis=dim)
    return value


def shifted(block, axis, distance):
    devices = range(lax.axis_size(axis))
    route = [(i - distance, i) for i in devices if i - distance in devices]
    return lax.ppermute(block, axis, route)


def band_advance(fields, coeffs, time_step):
    center = fields[:, :, 1:-1]
    along_x = fields[:, :, 2:] + fields[:, :, :-2]
    along_y = jnp.roll(center, 1, -2) + jnp.roll(center, -1, -2)
    along_z = jnp.roll(center, 1, -1) + jnp.roll(center, -1, -1)
    laplace_term = along_x + along_y + along_z - 6.0 * center
    substrate = center[:, 0]
    catalyst = center[:, 1]
    feed_values = coeffs[:, 0, 1:-1]
    kill_values = coeffs[:, 1, 1:-1]
    reaction = substrate * catalyst * catalyst
    new_sub = (
        substrate
        + spread_fast * laplace_term[:, 0]
        + time_step * (feed_values * (1.0 - substrate) - reaction)
    )
    new_cat = (
        catalyst
        + spread_slow * laplace_term[:, 1]
        + time_step * (reaction - (feed_values + kill_values) * catalyst)
    )
    return jnp.stack([new_sub, new_cat], axis=1)


def evolve(fields, padded_coeffs, time_step, repeats, padder, halo_width):
    total_width = padded_coeffs.shape[2]
    for outer_step in range(repeats // halo_width):
        fields = padder(fields)
        for inner_step in range(halo_width):
            fields = band_advance(
                fields, padded_coeffs[:, :, inner_step : total_width - inner_step], time_step
            )
    return fields


def capped_width(wanted, slab_rows, repeats):
    width = wanted
    while width > slab_rows or repeats % width != 0:
        width = width // 2
    return width


def restrict(values):
    leading = values.shape[:-3]
    sizes_x, sizes_y, sizes_z = values.shape[-3:]
    blocks = values.reshape(leading + (sizes_x // 2, 2, sizes_y // 2, 2, sizes_z // 2, 2))
    return jnp.mean(blocks, axis=(-5, -3, -1))


def prolong(values):
    return jnp.repeat(jnp.repeat(jnp.repeat(values, 2, -3), 2, -2), 2, -1)


def local(slice_ends, initial, feed_rate, kill_rate):
    slab_rows = feed_rate.shape[0]
    fine_width = capped_width(8, slab_rows, NF)
    coarse_width = capped_width(8, slab_rows // 2, KC)

    def fine_pad(values):
        return padded(values, (("space", 2),), fine_width)

    def coarse_pad(values):
        return padded(values, (("space", 2),), coarse_width)

    earlier = shifted(slice_ends[3], "tm", 1)
    first_start = jnp.where(lax.axis_index("tm") == 0, initial, earlier)
    starts = jnp.concatenate([first_start[None], slice_ends[0:3]], axis=0)
    coeffs = jnp.stack([feed_rate, kill_rate])[None]
    fine_ends = evolve(starts, fine_pad(coeffs), fine_step, NF, fine_pad, fine_width)
    coarse_coeffs = coarse_pad(restrict(coeffs))

    def coarse(fields):
        return evolve(fields, coarse_coeffs, coarse_step, KC, coarse_pad, coarse_width)

    target = restrict(fine_ends[3:4])
    launch = coarse(restrict(slice_ends[3:4]))
    quartets = lax.axis_size("tm")
    zero_field = jnp.zeros_like(target)

    def relay_turn(turn_index, offset):
        return shifted(coarse(target + offset) - launch, "tm", 1)

    correction = lax.fori_loop(0, quartets - 1, relay_turn, zero_field)
    return fine_ends + prolong(correction)


def solution(mesh):
    in_specs = (
        P("tm", None, "space", None, None),
        P(None, "space", None, None),
        P("space", None, None),
        P("space", None, None),
    )
    out_specs = P("tm", None, "space", None, None)
    return jax.shard_map(local, mesh=mesh, in_specs=in_specs, out_specs=out_specs, check_vma=False)
```

profile of v0, /device:TPU:0, one launch (start us, length us, event | category | flops | bytes accessed | tf_op | source)
XLA Modules:
  0.0 157.3 jit_solution(510470556876008915)
XLA Ops:
  0.0 0.9 fusion.380
  0.9 9.8 %reshape.2791 = f32[2,2,2,8,2,128,2]{6,5,4,3,2,1,0:T(8,128)} reshape(f32[1,2,4,16,256]{4,3,2,1,0:T(8,128)S(1)} %get-tuple-element.101) | data formatting | bytes 262144 | tf_op jit(solution)/shard_map/reshape | solution.py:80
  10.7 4.1 %reduce_sum.29 = f32[2,2,8,128]{3,2,1,0:T(8,128)S(1)} reduce(f32[2,2,2,8,2,128,2]{6,5,4,3,2,1,0:T(8,128)} %reshape.2791, f32[]{:T(128)} %constant.18.clone.1), dimensions={2,4,6}, to_apply=%region_2.3 | reduce | flops 28672 | bytes 147460 | tf_op jit(solution)/shard_map/reduce_sum | solution.py:81
  14.8 5.5 %collective-permute-start.18 = (f32[1,2,2,8,128]{4,3,2,1,0:T(8,128)S(1)}, f32[1,2,2,8,128]{4,3,2,1,0:T(8,128)S(1)}, u32[]{:S(2)}, u32[]{:S(2)}) collective-permute-start(f32[1,2,2,8,128]{4,3,2,1,0:T(8,128)S(1)} %multiply_bitcast_fusion), channel_id=1, source_target_pairs={{1,0},{2,1},{3,2},{4,3},{5,4},{6,5},{7,6},{8,7},{9,8},{10,9},{11,1... | collective-permute-start | bytes 49160 | tf_op jit(solution)/shard_map/ppermute | solution.py:24
  20.3 5.5 %stack.170 = f32[1,1,2,2,8,2,128,2]{7,6,5,4,3,2,1,0:T(8,128)} reshape(f32[4,16,256]{2,1,0:T(8,128)S(1)} %copy-done.2) | data formatting | bytes 131072 | tf_op jit(solution)/shard_map/stack | solution.py:102
  25.8 2.9 %copy.8 = f32[1,1,2,2,8,2,128,2]{6,4,7,5,3,2,1,0:T(8,128)S(1)} copy(f32[1,1,2,2,8,2,128,2]{7,6,5,4,3,2,1,0:T(8,128)} %stack.170) | data formatting | bytes 131072 | tf_op jit(solution)/shard_map/stack | solution.py:102
  28.7 5.5 %stack.171 = f32[1,1,2,2,8,2,128,2]{7,6,5,4,3,2,1,0:T(8,128)} reshape(f32[4,16,256]{2,1,0:T(8,128)S(1)} %copy-done.1) | data formatting | bytes 131072 | tf_op jit(solution)/shard_map/stack | solution.py:102
  34.2 2.8 %copy.9 = f32[1,1,2,2,8,2,128,2]{6,4,7,5,3,2,1,0:T(8,128)S(1)} copy(f32[1,1,2,2,8,2,128,2]{7,6,5,4,3,2,1,0:T(8,128)} %stack.171) | data formatting | bytes 131072 | tf_op jit(solution)/shard_map/stack | solution.py:102
  37.1 4.5 %collective-permute-start.10 = (f32[1,2,2,8,128]{4,3,2,1,0:T(8,128)S(1)}, f32[1,2,2,8,128]{4,3,2,1,0:T(8,128)S(1)}, u32[]{:S(2)}, u32[]{:S(2)}) collective-permute-start(f32[1,2,2,8,128]{4,3,2,1,0:T(8,128)S(1)} %multiply_bitcast_fusion.1), channel_id=1, source_target_pairs={{1,0},{2,1},{3,2},{4,3},{5,4},{6,5},{7,6},{8,7},{9,8},{10,9},{11,1... | collective-permute-start | bytes 49160 | tf_op jit(solution)/shard_map/ppermute | solution.py:24
  41.9 1.2 collective-permute-done.10
  43.1 4.4 %collective-permute-done.9 = f32[1,2,2,8,128]{4,3,2,1,0:T(8,128)S(1)} collective-permute-done((f32[1,2,2,8,128]{4,3,2,1,0:T(8,128)S(1)}, f32[1,2,2,8,128]{4,3,2,1,0:T(8,128)S(1)}, u32[]{:S(2)}, u32[]{:S(2)}) %collective-permute-start.9) | collective-permute-done | bytes 16416 | tf_op jit(solution)/shard_map/ppermute | solution.py:23
  47.9 0.5 collective-permute-start.19
  48.4 4.1 %collective-permute-start.4 = (f32[1,2,4,16,256]{4,3,2,1,0:T(8,128)S(1)}, f32[1,2,4,16,256]{4,3,2,1,0:T(8,128)S(1)}, u32[]{:S(2)}, u32[]{:S(2)}) collective-permute-start(f32[1,2,4,16,256]{4,3,2,1,0:T(8,128)S(1)} %maximum_bitcast_fusion), channel_id=1, source_target_pairs={{1,0},{2,1},{3,2},{4,3},{5,4},{6,5},{7,6},{8,7},{9,8},{10,9},{11,1... | collective-permute-start | bytes 393224 | tf_op jit(solution)/shard_map/ppermute | solution.py:24
  52.4 3.4 %collective-permute-start = (f32[2,4,16,256]{3,2,1,0:T(8,128)S(1)}, f32[2,4,16,256]{3,2,1,0:T(8,128)S(1)}, u32[]{:S(2)}, u32[]{:S(2)}) collective-permute-start(f32[2,4,16,256]{3,2,1,0:T(8,128)S(1)} %get-tuple-element.102), channel_id=1, source_target_pairs={{0,16},{1,17},{2,18},{3,19},{4,20},{5,21},{6,22},{7,23},{8,24},{9,... | collective-permute-start | bytes 393224 | tf_op jit(solution)/shard_map/ppermute | solution.py:32
  56.4 4.2 %collective-permute-start.22 = (f32[1,2,2,8,128]{4,3,2,1,0:T(8,128)S(1)}, f32[1,2,2,8,128]{4,3,2,1,0:T(8,128)S(1)}, u32[]{:S(2)}, u32[]{:S(2)}) collective-permute-start(f32[1,2,2,8,128]{4,3,2,1,0:T(8,128)S(1)} %pad_maximum_fusion.91), channel_id=1, source_target_pairs={{1,0},{2,1},{3,2},{4,3},{5,4},{6,5},{7,6},{8,7},{9,8},{10,9},{11,1... | collective-permute-start | bytes 49160 | tf_op jit(solution)/shard_map/ppermute | solution.py:24
  60.7 1.4 collective-permute-done.22
  62.1 4.4 %collective-permute-done.21 = f32[1,2,2,8,128]{4,3,2,1,0:T(8,128)S(1)} collective-permute-done((f32[1,2,2,8,128]{4,3,2,1,0:T(8,128)S(1)}, f32[1,2,2,8,128]{4,3,2,1,0:T(8,128)S(1)}, u32[]{:S(2)}, u32[]{:S(2)}) %collective-permute-start.21) | collective-permute-done | bytes 16416 | tf_op jit(solution)/shard_map/ppermute | solution.py:23
  67.1 0.5 collective-permute-start.23
  67.7 0.9 collective-permute-done.24
  68.6 4.5 %collective-permute-done.23 = f32[1,2,2,8,128]{4,3,2,1,0:T(8,128)S(1)} collective-permute-done((f32[1,2,2,8,128]{4,3,2,1,0:T(8,128)S(1)}, f32[1,2,2,8,128]{4,3,2,1,0:T(8,128)S(1)}, u32[]{:S(2)}, u32[]{:S(2)}) %collective-permute-start.23) | collective-permute-done | bytes 16416 | tf_op jit(solution)/shard_map/ppermute | solution.py:23
  73.4 0.5 collective-permute-start.1
  73.9 6.2 %collective-permute-done.2 = f32[4,2,4,16,256]{4,3,2,1,0:T(8,128)S(1)} collective-permute-done((f32[4,2,4,16,256]{4,3,2,1,0:T(8,128)S(1)}, f32[4,2,4,16,256]{4,3,2,1,0:T(8,128)S(1)}, u32[]{:S(2)}, u32[]{:S(2)}) %collective-permute-start.2) | collective-permute-done | bytes 524320 | tf_op jit(solution)/shard_map/ppermute | solution.py:24
  80.1 4.9 %collective-permute-done.1 = f32[4,2,4,16,256]{4,3,2,1,0:T(8,128)S(1)} collective-permute-done((f32[4,2,4,16,256]{4,3,2,1,0:T(8,128)S(1)}, f32[4,2,4,16,256]{4,3,2,1,0:T(8,128)S(1)}, u32[]{:S(2)}, u32[]{:S(2)}) %collective-permute-start.1) | collective-permute-done | bytes 524320 | tf_op jit(solution)/shard_map/ppermute | solution.py:23
  85.4 0.3 fusion.379
  85.7 0.5 fusion.377
  86.2 1.5 fusion.6
  87.6 0.4 fusion.61
  88.5 0.4 fusion.31
  88.9 0.8 fusion.26
  89.7 0.3 fusion.96
  90.4 0.3 fusion.53
  90.7 0.6 fusion.48
  92.1 0.4 fusion.79
  92.8 3.6 %collective-permute-start.5 = (f32[4,2,4,16,256]{4,3,2,1,0:T(8,128)S(1)}, f32[4,2,4,16,256]{4,3,2,1,0:T(8,128)S(1)}, u32[]{:S(2)}, u32[]{:S(2)}) collective-permute-start(f32[4,2,4,16,256]{4,3,2,1,0:T(8,128)S(1)} %pad_maximum_fusion.22), channel_id=1, source_target_pairs={{0,1},{1,2},{2,3},{3,4},{4,5},{5,6},{6,7},{7,8},{8,9},{9,10},{10,1... | collective-permute-start | bytes 1572872 | tf_op jit(solution)/shard_map/ppermute | solution.py:23
  96.5 3.0 %collective-permute-done.6 = f32[4,2,4,16,256]{4,3,2,1,0:T(8,128)S(1)} collective-permute-done((f32[4,2,4,16,256]{4,3,2,1,0:T(8,128)S(1)}, f32[4,2,4,16,256]{4,3,2,1,0:T(8,128)S(1)}, u32[]{:S(2)}, u32[]{:S(2)}) %collective-permute-start.6) | collective-permute-done | bytes 524320 | tf_op jit(solution)/shard_map/ppermute | solution.py:24
  99.4 5.0 %collective-permute-done.5 = f32[4,2,4,16,256]{4,3,2,1,0:T(8,128)S(1)} collective-permute-done((f32[4,2,4,16,256]{4,3,2,1,0:T(8,128)S(1)}, f32[4,2,4,16,256]{4,3,2,1,0:T(8,128)S(1)}, u32[]{:S(2)}, u32[]{:S(2)}) %collective-permute-start.5) | collective-permute-done | bytes 524320 | tf_op jit(solution)/shard_map/ppermute | solution.py:23
  104.8 0.3 fusion.376
  105.1 0.5 fusion.374
  105.6 1.5 fusion
  107.0 0.4 fusion.57
  107.9 0.4 fusion.21
  108.3 0.8 fusion.16
  109.1 0.3 fusion.91
  109.8 0.3 fusion.43
  110.1 0.6 fusion.38
  111.4 0.4 fusion.69
  112.1 9.8 %reshape.2790 = f32[2,2,2,8,2,128,2]{6,5,4,3,2,1,0:T(8,128)} reshape(f32[1,2,4,16,256]{4,3,2,1,0:T(8,128)S(1)} %fusion.124) | data formatting | bytes 262144 | tf_op jit(solution)/shard_map/reshape | solution.py:80
  121.9 4.0 %reduce_sum.27 = f32[2,2,8,128]{3,2,1,0:T(8,128)S(1)} reduce(f32[2,2,2,8,2,128,2]{6,5,4,3,2,1,0:T(8,128)} %reshape.2790, f32[]{:T(128)} %constant.18.clone.1), dimensions={2,4,6}, to_apply=%region_0.1 | reduce | flops 28672 | bytes 147460 | tf_op jit(solution)/shard_map/reduce_sum | solution.py:81
  126.0 5.4 %collective-permute-start.7 = (f32[1,2,2,8,128]{4,3,2,1,0:T(8,128)S(1)}, f32[1,2,2,8,128]{4,3,2,1,0:T(8,128)S(1)}, u32[]{:S(2)}, u32[]{:S(2)}) collective-permute-start(f32[1,2,2,8,128]{4,3,2,1,0:T(8,128)S(1)} %multiply_bitcast_fusion.2), channel_id=1, source_target_pairs={{0,1},{1,2},{2,3},{3,4},{4,5},{5,6},{6,7},{7,8},{8,9},{9,10},{10,1... | collective-permute-start | bytes 49160 | tf_op jit(solution)/shard_map/while/body/eval_jaxpr/ppermute | solution.py:23
  131.5 0.5 collective-permute-done.8
  133.0 2.3 %collective-permute-start.11 = (f32[1,2,2,8,128]{4,3,2,1,0:T(8,128)S(1)}, f32[1,2,2,8,128]{4,3,2,1,0:T(8,128)S(1)}, u32[]{:S(2)}, u32[]{:S(2)}) collective-permute-start(f32[1,2,2,8,128]{4,3,2,1,0:T(8,128)S(1)} %pad_maximum_fusion.87), channel_id=1, source_target_pairs={{0,1},{1,2},{2,3},{3,4},{4,5},{5,6},{6,7},{7,8},{8,9},{9,10},{10,1... | collective-permute-start | bytes 49160 | tf_op jit(solution)/shard_map/while/body/eval_jaxpr/ppermute | solution.py:23
  135.3 0.6 collective-permute-done.12
  135.9 3.0 %collective-permute-done.11 = f32[1,2,2,8,128]{4,3,2,1,0:T(8,128)S(1)} collective-permute-done((f32[1,2,2,8,128]{4,3,2,1,0:T(8,128)S(1)}, f32[1,2,2,8,128]{4,3,2,1,0:T(8,128)S(1)}, u32[]{:S(2)}, u32[]{:S(2)}) %collective-permute-start.11) | collective-permute-done | bytes 16416 | tf_op jit(solution)/shard_map/while/body/eval_jaxpr/ppermute | solution.py:23
  139.5 0.5 collective-permute-start.13
  140.0 0.9 collective-permute-done.14
  140.9 4.5 %collective-permute-done.13 = f32[1,2,2,8,128]{4,3,2,1,0:T(8,128)S(1)} collective-permute-done((f32[1,2,2,8,128]{4,3,2,1,0:T(8,128)S(1)}, f32[1,2,2,8,128]{4,3,2,1,0:T(8,128)S(1)}, u32[]{:S(2)}, u32[]{:S(2)}) %collective-permute-start.13) | collective-permute-done | bytes 16416 | tf_op jit(solution)/shard_map/while/body/eval_jaxpr/ppermute | solution.py:23
  146.0 0.5 collective-permute-start.15
  146.5 0.9 collective-permute-done.16
  147.5 4.5 %collective-permute-done.15 = f32[1,2,2,8,128]{4,3,2,1,0:T(8,128)S(1)} collective-permute-done((f32[1,2,2,8,128]{4,3,2,1,0:T(8,128)S(1)}, f32[1,2,2,8,128]{4,3,2,1,0:T(8,128)S(1)}, u32[]{:S(2)}, u32[]{:S(2)}) %collective-permute-start.15) | collective-permute-done | bytes 16416 | tf_op jit(solution)/shard_map/while/body/eval_jaxpr/ppermute | solution.py:23
  152.5 1.6 collective-permute-start.25
  154.1 1.4 collective-permute-done.25
  155.8 0.4 broadcast_in_dim.28
  156.1 0.3 copy.11
  156.4 0.9 fusion.64
  (176 shorter events, 9.6 us)
Async XLA Ops:
  10.7 9.6 %copy-start.2 = (f32[4,16,256]{2,1,0:T(8,128)S(1)}, f32[4,16,256]{2,1,0:T(8,128)}, u32[]{:S(2)}) copy-start(f32[4,16,256]{2,1,0:T(8,128)} %param.6) | copy-start | bytes 196612
  14.8 26.8 %collective-permute-start.18 = (f32[1,2,2,8,128]{4,3,2,1,0:T(8,128)S(1)}, f32[1,2,2,8,128]{4,3,2,1,0:T(8,128)S(1)}, u32[]{:S(2)}, u32[]{:S(2)}) collective-permute-start(f32[1,2,2,8,128]{4,3,2,1,0:T(8,128)S(1)} %multiply_bitcast_fusion), channel_id=1, source_target_pairs={{1,0},{2,1},{3,2},{4,3},{5,4},{6,5},{7,6},{8,7},{9,8},{10,9},{11,1... | collective-permute-start | bytes 49160 | tf_op jit(solution)/shard_map/ppermute | solution.py:24
  20.3 21.3 %collective-permute-start.17 = (f32[1,2,2,8,128]{4,3,2,1,0:T(8,128)S(1)}, f32[1,2,2,8,128]{4,3,2,1,0:T(8,128)S(1)}, u32[]{:S(2)}, u32[]{:S(2)}) collective-permute-start(f32[1,2,2,8,128]{4,3,2,1,0:T(8,128)S(1)} %multiply_bitcast_fusion), channel_id=1, source_target_pairs={{0,1},{1,2},{2,3},{3,4},{4,5},{5,6},{6,7},{7,8},{8,9},{9,10},{10,1... | collective-permute-start | bytes 49160 | tf_op jit(solution)/shard_map/ppermute | solution.py:23
  25.8 2.9 %copy-start.1 = (f32[4,16,256]{2,1,0:T(8,128)S(1)}, f32[4,16,256]{2,1,0:T(8,128)}, u32[]{:S(2)}) copy-start(f32[4,16,256]{2,1,0:T(8,128)} %param.7) | copy-start | bytes 196612
  37.1 5.9 %collective-permute-start.10 = (f32[1,2,2,8,128]{4,3,2,1,0:T(8,128)S(1)}, f32[1,2,2,8,128]{4,3,2,1,0:T(8,128)S(1)}, u32[]{:S(2)}, u32[]{:S(2)}) collective-permute-start(f32[1,2,2,8,128]{4,3,2,1,0:T(8,128)S(1)} %multiply_bitcast_fusion.1), channel_id=1, source_target_pairs={{1,0},{2,1},{3,2},{4,3},{5,4},{6,5},{7,6},{8,7},{9,8},{10,9},{11,1... | collective-permute-start | bytes 49160 | tf_op jit(solution)/shard_map/ppermute | solution.py:24
  41.6 5.9 %collective-permute-start.9 = (f32[1,2,2,8,128]{4,3,2,1,0:T(8,128)S(1)}, f32[1,2,2,8,128]{4,3,2,1,0:T(8,128)S(1)}, u32[]{:S(2)}, u32[]{:S(2)}) collective-permute-start(f32[1,2,2,8,128]{4,3,2,1,0:T(8,128)S(1)} %multiply_bitcast_fusion.1), channel_id=1, source_target_pairs={{0,1},{1,2},{2,3},{3,4},{4,5},{5,6},{6,7},{7,8},{8,9},{9,10},{10,1... | collective-permute-start | bytes 49160 | tf_op jit(solution)/shard_map/ppermute | solution.py:23
  47.8 8.0 %collective-permute-start.20 = (f32[1,2,2,8,128]{4,3,2,1,0:T(8,128)S(1)}, f32[1,2,2,8,128]{4,3,2,1,0:T(8,128)S(1)}, u32[]{:S(2)}, u32[]{:S(2)}) collective-permute-start(f32[1,2,2,8,128]{4,3,2,1,0:T(8,128)S(1)} %pad_maximum_fusion.90), channel_id=1, source_target_pairs={{1,0},{2,1},{3,2},{4,3},{5,4},{6,5},{7,6},{8,7},{9,8},{10,9},{11,1... | collective-permute-start | bytes 49160 | tf_op jit(solution)/shard_map/ppermute | solution.py:24
  47.9 8.0 %collective-permute-start.19 = (f32[1,2,2,8,128]{4,3,2,1,0:T(8,128)S(1)}, f32[1,2,2,8,128]{4,3,2,1,0:T(8,128)S(1)}, u32[]{:S(2)}, u32[]{:S(2)}) collective-permute-start(f32[1,2,2,8,128]{4,3,2,1,0:T(8,128)S(1)} %pad_maximum_fusion.90), channel_id=1, source_target_pairs={{0,1},{1,2},{2,3},{3,4},{4,5},{5,6},{6,7},{7,8},{8,9},{9,10},{10,1... | collective-permute-start | bytes 49160 | tf_op jit(solution)/shard_map/ppermute | solution.py:23
  48.4 24.7 %collective-permute-start.4 = (f32[1,2,4,16,256]{4,3,2,1,0:T(8,128)S(1)}, f32[1,2,4,16,256]{4,3,2,1,0:T(8,128)S(1)}, u32[]{:S(2)}, u32[]{:S(2)}) collective-permute-start(f32[1,2,4,16,256]{4,3,2,1,0:T(8,128)S(1)} %maximum_bitcast_fusion), channel_id=1, source_target_pairs={{1,0},{2,1},{3,2},{4,3},{5,4},{6,5},{7,6},{8,7},{9,8},{10,9},{11,1... | collective-permute-start | bytes 393224 | tf_op jit(solution)/shard_map/ppermute | solution.py:24
  52.4 20.6 %collective-permute-start.3 = (f32[1,2,4,16,256]{4,3,2,1,0:T(8,128)S(1)}, f32[1,2,4,16,256]{4,3,2,1,0:T(8,128)S(1)}, u32[]{:S(2)}, u32[]{:S(2)}) collective-permute-start(f32[1,2,4,16,256]{4,3,2,1,0:T(8,128)S(1)} %maximum_bitcast_fusion), channel_id=1, source_target_pairs={{0,1},{1,2},{2,3},{3,4},{4,5},{5,6},{6,7},{7,8},{8,9},{9,10},{10,1... | collective-permute-start | bytes 393224 | tf_op jit(solution)/shard_map/ppermute | solution.py:23
  52.4 20.8 %collective-permute-start = (f32[2,4,16,256]{3,2,1,0:T(8,128)S(1)}, f32[2,4,16,256]{3,2,1,0:T(8,128)S(1)}, u32[]{:S(2)}, u32[]{:S(2)}) collective-permute-start(f32[2,4,16,256]{3,2,1,0:T(8,128)S(1)} %get-tuple-element.102), channel_id=1, source_target_pairs={{0,16},{1,17},{2,18},{3,19},{4,20},{5,21},{6,22},{7,23},{8,24},{9,... | collective-permute-start | bytes 393224 | tf_op jit(solution)/shard_map/ppermute | solution.py:32
  56.0 11.6 %copy-start = (f32[4,2,4,16,256]{4,3,2,1,0:T(8,128)S(1)}, f32[4,2,4,16,256]{4,3,2,1,0:T(8,128)}, u32[]{:S(2)}) copy-start(f32[4,2,4,16,256]{4,3,2,1,0:T(8,128)} %param.4) | copy-start | bytes 1572868
  56.4 5.7 %collective-permute-start.22 = (f32[1,2,2,8,128]{4,3,2,1,0:T(8,128)S(1)}, f32[1,2,2,8,128]{4,3,2,1,0:T(8,128)S(1)}, u32[]{:S(2)}, u32[]{:S(2)}) collective-permute-start(f32[1,2,2,8,128]{4,3,2,1,0:T(8,128)S(1)} %pad_maximum_fusion.91), channel_id=1, source_target_pairs={{1,0},{2,1},{3,2},{4,3},{5,4},{6,5},{7,6},{8,7},{9,8},{10,9},{11,1... | collective-permute-start | bytes 49160 | tf_op jit(solution)/shard_map/ppermute | solution.py:24
  60.6 5.9 %collective-permute-start.21 = (f32[1,2,2,8,128]{4,3,2,1,0:T(8,128)S(1)}, f32[1,2,2,8,128]{4,3,2,1,0:T(8,128)S(1)}, u32[]{:S(2)}, u32[]{:S(2)}) collective-permute-start(f32[1,2,2,8,128]{4,3,2,1,0:T(8,128)S(1)} %pad_maximum_fusion.91), channel_id=1, source_target_pairs={{0,1},{1,2},{2,3},{3,4},{4,5},{5,6},{6,7},{7,8},{8,9},{9,10},{10,1... | collective-permute-start | bytes 49160 | tf_op jit(solution)/shard_map/ppermute | solution.py:23
  67.1 1.5 collective-permute-start.24
  67.1 5.9 %collective-permute-start.23 = (f32[1,2,2,8,128]{4,3,2,1,0:T(8,128)S(1)}, f32[1,2,2,8,128]{4,3,2,1,0:T(8,128)S(1)}, u32[]{:S(2)}, u32[]{:S(2)}) collective-permute-start(f32[1,2,2,8,128]{4,3,2,1,0:T(8,128)S(1)} %pad_maximum_fusion.92), channel_id=1, source_target_pairs={{0,1},{1,2},{2,3},{3,4},{4,5},{5,6},{6,7},{7,8},{8,9},{9,10},{10,1... | collective-permute-start | bytes 49160 | tf_op jit(solution)/shard_map/ppermute | solution.py:23
  67.7 5.5 %copy-start.3 = (f32[2,4,16,256]{3,2,1,0:T(8,128)S(1)}, f32[2,4,16,256]{3,2,1,0:T(8,128)}, u32[]{:S(2)}) copy-start(f32[2,4,16,256]{3,2,1,0:T(8,128)} %param.5) | copy-start | bytes 393220
  73.3 6.8 %collective-permute-start.2 = (f32[4,2,4,16,256]{4,3,2,1,0:T(8,128)S(1)}, f32[4,2,4,16,256]{4,3,2,1,0:T(8,128)S(1)}, u32[]{:S(2)}, u32[]{:S(2)}) collective-permute-start(f32[4,2,4,16,256]{4,3,2,1,0:T(8,128)S(1)} %pad_maximum_fusion.21), channel_id=1, source_target_pairs={{1,0},{2,1},{3,2},{4,3},{5,4},{6,5},{7,6},{8,7},{9,8},{10,9},{11,1... | collective-permute-start | bytes 1572872 | tf_op jit(solution)/shard_map/ppermute | solution.py:24
  73.4 11.6 %collective-permute-start.1 = (f32[4,2,4,16,256]{4,3,2,1,0:T(8,128)S(1)}, f32[4,2,4,16,256]{4,3,2,1,0:T(8,128)S(1)}, u32[]{:S(2)}, u32[]{:S(2)}) collective-permute-start(f32[4,2,4,16,256]{4,3,2,1,0:T(8,128)S(1)} %pad_maximum_fusion.21), channel_id=1, source_target_pairs={{0,1},{1,2},{2,3},{3,4},{4,5},{5,6},{6,7},{7,8},{8,9},{9,10},{10,1... | collective-permute-start | bytes 1572872 | tf_op jit(solution)/shard_map/ppermute | solution.py:23
  92.7 6.8 %collective-permute-start.6 = (f32[4,2,4,16,256]{4,3,2,1,0:T(8,128)S(1)}, f32[4,2,4,16,256]{4,3,2,1,0:T(8,128)S(1)}, u32[]{:S(2)}, u32[]{:S(2)}) collective-permute-start(f32[4,2,4,16,256]{4,3,2,1,0:T(8,128)S(1)} %pad_maximum_fusion.22), channel_id=1, source_target_pairs={{1,0},{2,1},{3,2},{4,3},{5,4},{6,5},{7,6},{8,7},{9,8},{10,9},{11,1... | collective-permute-start | bytes 1572872 | tf_op jit(solution)/shard_map/ppermute | solution.py:24
  92.8 11.7 %collective-permute-start.5 = (f32[4,2,4,16,256]{4,3,2,1,0:T(8,128)S(1)}, f32[4,2,4,16,256]{4,3,2,1,0:T(8,128)S(1)}, u32[]{:S(2)}, u32[]{:S(2)}) collective-permute-start(f32[4,2,4,16,256]{4,3,2,1,0:T(8,128)S(1)} %pad_maximum_fusion.22), channel_id=1, source_target_pairs={{0,1},{1,2},{2,3},{3,4},{4,5},{5,6},{6,7},{7,8},{8,9},{9,10},{10,1... | collective-permute-start | bytes 1572872 | tf_op jit(solution)/shard_map/ppermute | solution.py:23
  125.9 6.1 %collective-permute-start.8 = (f32[1,2,2,8,128]{4,3,2,1,0:T(8,128)S(1)}, f32[1,2,2,8,128]{4,3,2,1,0:T(8,128)S(1)}, u32[]{:S(2)}, u32[]{:S(2)}) collective-permute-start(f32[1,2,2,8,128]{4,3,2,1,0:T(8,128)S(1)} %multiply_bitcast_fusion.2), channel_id=1, source_target_pairs={{1,0},{2,1},{3,2},{4,3},{5,4},{6,5},{7,6},{8,7},{9,8},{10,9},{11,1... | collective-permute-start | bytes 49160 | tf_op jit(solution)/shard_map/while/body/eval_jaxpr/ppermute | solution.py:24
  126.0 6.2 %collective-permute-start.7 = (f32[1,2,2,8,128]{4,3,2,1,0:T(8,128)S(1)}, f32[1,2,2,8,128]{4,3,2,1,0:T(8,128)S(1)}, u32[]{:S(2)}, u32[]{:S(2)}) collective-permute-start(f32[1,2,2,8,128]{4,3,2,1,0:T(8,128)S(1)} %multiply_bitcast_fusion.2), channel_id=1, source_target_pairs={{0,1},{1,2},{2,3},{3,4},{4,5},{5,6},{6,7},{7,8},{8,9},{9,10},{10,1... | collective-permute-start | bytes 49160 | tf_op jit(solution)/shard_map/while/body/eval_jaxpr/ppermute | solution.py:23
  132.9 3.0 %collective-permute-start.12 = (f32[1,2,2,8,128]{4,3,2,1,0:T(8,128)S(1)}, f32[1,2,2,8,128]{4,3,2,1,0:T(8,128)S(1)}, u32[]{:S(2)}, u32[]{:S(2)}) collective-permute-start(f32[1,2,2,8,128]{4,3,2,1,0:T(8,128)S(1)} %pad_maximum_fusion.87), channel_id=1, source_target_pairs={{1,0},{2,1},{3,2},{4,3},{5,4},{6,5},{7,6},{8,7},{9,8},{10,9},{11,1... | collective-permute-start | bytes 49160 | tf_op jit(solution)/shard_map/while/body/eval_jaxpr/ppermute | solution.py:24
  133.0 5.9 %collective-permute-start.11 = (f32[1,2,2,8,128]{4,3,2,1,0:T(8,128)S(1)}, f32[1,2,2,8,128]{4,3,2,1,0:T(8,128)S(1)}, u32[]{:S(2)}, u32[]{:S(2)}) collective-permute-start(f32[1,2,2,8,128]{4,3,2,1,0:T(8,128)S(1)} %pad_maximum_fusion.87), channel_id=1, source_target_pairs={{0,1},{1,2},{2,3},{3,4},{4,5},{5,6},{6,7},{7,8},{8,9},{9,10},{10,1... | collective-permute-start | bytes 49160 | tf_op jit(solution)/shard_map/while/body/eval_jaxpr/ppermute | solution.py:23
  139.4 1.5 collective-permute-start.14
  139.5 5.9 %collective-permute-start.13 = (f32[1,2,2,8,128]{4,3,2,1,0:T(8,128)S(1)}, f32[1,2,2,8,128]{4,3,2,1,0:T(8,128)S(1)}, u32[]{:S(2)}, u32[]{:S(2)}) collective-permute-start(f32[1,2,2,8,128]{4,3,2,1,0:T(8,128)S(1)} %pad_maximum_fusion.88), channel_id=1, source_target_pairs={{0,1},{1,2},{2,3},{3,4},{4,5},{5,6},{6,7},{7,8},{8,9},{9,10},{10,1... | collective-permute-start | bytes 49160 | tf_op jit(solution)/shard_map/while/body/eval_jaxpr/ppermute | solution.py:23
  146.0 1.5 collective-permute-start.16
  146.0 5.9 %collective-permute-start.15 = (f32[1,2,2,8,128]{4,3,2,1,0:T(8,128)S(1)}, f32[1,2,2,8,128]{4,3,2,1,0:T(8,128)S(1)}, u32[]{:S(2)}, u32[]{:S(2)}) collective-permute-start(f32[1,2,2,8,128]{4,3,2,1,0:T(8,128)S(1)} %pad_maximum_fusion.89), channel_id=1, source_target_pairs={{0,1},{1,2},{2,3},{3,4},{4,5},{5,6},{6,7},{7,8},{8,9},{9,10},{10,1... | collective-permute-start | bytes 49160 | tf_op jit(solution)/shard_map/while/body/eval_jaxpr/ppermute | solution.py:23
  152.5 3.0 %collective-permute-start.25 = (f32[1,2,2,8,128]{4,3,2,1,0:T(8,128)S(1)}, f32[1,2,2,8,128]{4,3,2,1,0:T(8,128)S(1)}, u32[]{:S(2)}, u32[]{:S(2)}) collective-permute-start(f32[1,2,2,8,128]{4,3,2,1,0:T(8,128)S(1)} %maximum_subtract_fusion), channel_id=1, source_target_pairs={{0,16},{1,17},{2,18},{3,19},{4,20},{5,21},{6,22},{7,23},{8,24},{9,... | collective-permute-start | bytes 49160 | tf_op jit(solution)/shard_map/while/body/eval_jaxpr/ppermute | solution.py:32
where the time goes:
time: 158 us; the launch traced here: 157 us
  waiting for transfers between devices  52.4 us (33%)
  local copies, waits for them, and re-layouts  41.5 us (26%)
  starting transfers between devices  37.5 us (24%)
  other arithmetic  25 us (16%)
    ppermute x12, waiting for transfers between devices, padded(): before = lax.ppermute(last, axis, up)  35.3 us
    reshape x2, local copies, waits for them, and re-layouts, restrict(): values.reshape(leading + (sizes_x // 2, 2, sizes_y // 2, 2, sizes_z // 2,...  19.6 us
    ppermute x12, starting transfers between devices, padded(): after = lax.ppermute(initial, axis, down)  18.8 us
    another operation x4, local copies, waits for them, and re-layouts, local(): coeffs = jnp.stack([feed_rate, kill_rate])[None]  16.7 us
    ppermute x12, waiting for transfers between devices, padded(): after = lax.ppermute(initial, axis, down)  15.6 us
    ppermute x12, starting transfers between devices, padded(): before = lax.ppermute(last, axis, up)  13.7 us
    reduce_sum x3, other arithmetic, restrict(): return jnp.mean(blocks, axis=(-5, -3, -1))  8.1 us
    sub x24, other arithmetic, band_advance(): laplace_term = along_x + along_y + along_z - 6.0 * center  8.04 us
  transfers between devices with their start and end apart: 26, of which 19 were waited for; matrix products, arithmetic and copies ran while one was open for 12% of the time, Pallas kernels for 0%

commit v1 on v0

v1 whole, which is shorter than its diff:
```python
import jax
import jax.numpy as jnp
import numpy as np
from jax import lax
from jax.experimental import pallas as pl
from jax.experimental.pallas import tpu as pltpu
from jax.sharding import PartitionSpec as P

NF = 8
KC = 8

spread_fast = 0.14
spread_slow = 0.07
fine_step = 0.25
coarse_step = 1.0

LANES = 128
CHUNKS = ((3,), (2, 1), (0,))

VMEM = pl.BlockSpec(memory_space=pltpu.VMEM)
SMEM = pl.BlockSpec(memory_space=pltpu.SMEM)


def head_block(shape):
    return pl.BlockSpec((1,) + tuple(shape[1:]), lambda i: (0,) * len(shape))


def whole_block(shape):
    return pl.BlockSpec(tuple(shape), lambda i: (0,) * len(shape))


def step_plane(read, coeffs, row):
    h_feed = coeffs(0, row)
    h_loss = coeffs(1, row)
    height, width = h_feed.shape
    out = []
    planes = [read(0, row), read(1, row)]
    sums = []
    for field in (0, 1):
        center = planes[field]
        total = read(field, row + 1) + read(field, row - 1)
        total = total + (pltpu.roll(center, 1, 0) + pltpu.roll(center, height - 1, 0))
        total = total + (pltpu.roll(center, 1, 1) + pltpu.roll(center, width - 1, 1))
        sums.append(total)
    return planes, sums, h_feed, h_loss


def advance_plane(read, coeffs, row, time_step):
    (substrate, catalyst), (sum_u, sum_v), h_feed, h_loss = step_plane(read, coeffs, row)
    reaction = (time_step * substrate) * (catalyst * catalyst)
    new_u = (1.0 - 6.0 * spread_fast) * substrate + spread_fast * sum_u + (h_feed * (1.0 - substrate) - reaction)
    new_v = (1.0 - 6.0 * spread_slow) * catalyst + spread_slow * sum_v + (reaction - h_loss * catalyst)
    return new_u, new_v


def pool_matrix(width):
    matrix = np.zeros((width, width // 2), np.float32)
    matrix[np.arange(width), np.arange(width) // 2] = 1.0
    return matrix


def restrict_planes(load, n_fields, rows, scratch, pool):
    halves = []
    for field in range(n_fields):
        for pair in range(rows // 2):
            slot = field * (rows // 2) + pair
            plane = load(field, 2 * pair) + load(field, 2 * pair + 1)
            half = plane.shape[0] // 2
            lanes = []
            for at in range(plane.shape[1] // LANES):
                spot = slot * (plane.shape[1] // LANES) + at
                scratch[spot] = plane[:, at * LANES : (at + 1) * LANES]
                lanes.append(scratch[spot, pl.ds(0, half, 2), :] + scratch[spot, pl.ds(1, half, 2), :])
            halves.append(jnp.concatenate(lanes, axis=1))
    stacked = jnp.concatenate(halves, axis=0)
    pooled = jnp.dot(stacked, pool, precision=lax.Precision.HIGHEST, preferred_element_type=jnp.float32)
    return pooled * 0.125


def fine_kernel(n, rows, steps, with_coarse):
    def kernel(parity, *refs):
        refs = list(refs)
        own_c, inn_c, out_c, own, inn, out = refs[:6]
        refs = refs[6:]
        pool = refs.pop(0) if with_coarse else None
        result = refs.pop(0)
        coarse_out = refs.pop(0) if with_coarse else None
        coef, ping, pong = refs[:3]
        scratch = refs[3] if with_coarse else None
        odd = parity[0]

        def gather_coef(low, high):
            feed = jnp.concatenate([low[0, 0], own_c[0, 0], high[0, 0]], axis=0)
            kill = jnp.concatenate([low[0, 1], own_c[0, 1], high[0, 1]], axis=0)
            coef[0] = fine_step * feed
            coef[1] = fine_step * (feed + kill)

        @pl.when(odd == 0)
        def _():
            gather_coef(out_c, inn_c)

        @pl.when(odd == 1)
        def _():
            gather_coef(inn_c, out_c)

        shift = own.shape[0] - n

        def one_slice(index, carry):
            source = index + shift
            ping[:, rows : 2 * rows] = own[source]

            @pl.when(odd == 0)
            def _():
                ping[:, 0:rows] = out[source]
                ping[:, 2 * rows : 3 * rows] = inn[source]

            @pl.when(odd == 1)
            def _():
                ping[:, 0:rows] = inn[source]
                ping[:, 2 * rows : 3 * rows] = out[source]

            buffers = (ping, pong)
            for step in range(steps):
                src, dst = buffers[step % 2], buffers[(step + 1) % 2]
                first = rows - steps + 1 + step
                last = 3 * rows - first
                for row in range(first, last):
                    new_u, new_v = advance_plane(
                        lambda field, r: src[field, r], lambda which, r: coef[which, r], row, fine_step
                    )
                    if step == steps - 1:
                        result[index, 0, row - rows] = new_u
                        result[index, 1, row - rows] = new_v
                    else:
                        dst[0, row] = new_u
                        dst[1, row] = new_v
            return carry

        lax.fori_loop(0, n, one_slice, 0)
        if with_coarse:
            pooled = restrict_planes(lambda f, r: result[0, f, r], 2, rows, scratch, pool[...])
            coarse_out[...] = pooled.reshape(coarse_out.shape)

    return kernel


def fine_call(parity, coeff_parts, parts, n, steps, with_coarse):
    rows, sy, sz = parts[0].shape[-3:]
    state = (n, 2, rows, sy, sz)
    operands = [parity, *coeff_parts, *parts]
    in_specs = [SMEM] + [head_block(c.shape) for c in coeff_parts] + [whole_block(p.shape) for p in parts]
    out_shape = [jax.ShapeDtypeStruct(state, jnp.float32)]
    out_specs = [whole_block(state)]
    scratch = [
        pltpu.VMEM((2, 3 * rows, sy, sz), jnp.float32),
        pltpu.VMEM((2, 3 * rows, sy, sz), jnp.float32),
        pltpu.VMEM((2, 3 * rows, sy, sz), jnp.float32),
    ]
    if with_coarse:
        pool = jnp.asarray(pool_matrix(sz))
        operands.append(pool)
        in_specs.append(whole_block(pool.shape))
        coarse = (2, rows // 2, sy // 2, sz // 2)
        out_shape.append(jax.ShapeDtypeStruct(coarse, jnp.float32))
        out_specs.append(whole_block(coarse))
        scratch.append(pltpu.VMEM((rows * sz // LANES, sy, LANES), jnp.float32))
    return pl.pallas_call(
        fine_kernel(n, rows, steps, with_coarse),
        grid=(1,),
        in_specs=in_specs,
        out_specs=out_specs,
        out_shape=out_shape,
        scratch_shapes=scratch,
        name="fine",
    )(*operands)


def early_kernel(feed, kill, last, pool, result, scratch):
    rows = feed.shape[0]

    def load(field, row):
        return (last[0, 0, row], last[0, 1, row], feed[row], kill[row])[field]

    pooled = restrict_planes(load, 4, rows, scratch, pool[...])
    result[...] = pooled.reshape(result.shape)


def early_call(slice_ends, feed_rate, kill_rate):
    count = slice_ends.shape[0]
    rows, sy, sz = feed_rate.shape
    pool = jnp.asarray(pool_matrix(sz))
    last = pl.BlockSpec((1,) + slice_ends.shape[1:], lambda i: (count - 1, 0, 0, 0, 0))
    shape = (4, rows // 2, sy // 2, sz // 2)
    return pl.pallas_call(
        early_kernel,
        grid=(1,),
        in_specs=[whole_block(feed_rate.shape), whole_block(kill_rate.shape), last, whole_block(pool.shape)],
        out_specs=whole_block(shape),
        out_shape=jax.ShapeDtypeStruct(shape, jnp.float32),
        scratch_shapes=[pltpu.VMEM((2 * rows * sz // LANES, sy, LANES), jnp.float32)],
        name="early",
    )(feed_rate, kill_rate, slice_ends, pool)


def coarse_solve(targets, launches, coef, ping, pong, rows):
    blocks = len(targets)
    total = blocks * rows
    for b in range(blocks):
        for r in range(rows):
            feed = coarse_step * launches[b][2, r]
            coef[0, b * rows + r] = feed
            coef[1, b * rows + r] = feed + coarse_step * launches[b][3, r]
            for field in (0, 1):
                ping[0, field, b * rows + r] = targets[b][field, r]
                ping[1, field, b * rows + r] = launches[b][field, r]
    middle = (blocks // 2) * rows
    buffers = (ping, pong)
    ends = []
    for step in range(KC):
        src, dst = buffers[step % 2], buffers[(step + 1) % 2]
        reach = KC - 1 - step
        for state in (0, 1):
            for row in range(middle - reach, middle + rows + reach):
                new_u, new_v = advance_plane(
                    lambda field, r: src[state, field, r], lambda which, r: coef[which, r], row, coarse_step
                )
                dst[state, 0, row] = new_u
                dst[state, 1, row] = new_v
    final = buffers[KC % 2]
    return [final[0, f, middle + r] - final[1, f, middle + r] for f in (0, 1) for r in range(rows)]


def coarse_kernel(blocks):
    def kernel(place, *refs):
        targets, launches = refs[:blocks], refs[blocks : 2 * blocks]
        result, coef, ping, pong = refs[2 * blocks :]
        rows = result.shape[1]
        keep = jnp.where(place[1] > 0, 1.0, 0.0)
        planes = coarse_solve(targets, launches, coef, ping, pong, rows)
        for i, plane in enumerate(planes):
            result[i // rows, i % rows] = plane * keep

    return kernel


def coarse_scratch(blocks, block):
    _, rows, sy, sz = block
    return [
        pltpu.VMEM((2, blocks * rows, sy, sz), jnp.float32),
        pltpu.VMEM((2, 2, blocks * rows, sy, sz), jnp.float32),
        pltpu.VMEM((2, 2, blocks * rows, sy, sz), jnp.float32),
    ]


def coarse_call(place, targets, launches):
    blocks = len(targets)
    shape = targets[0].shape
    return pl.pallas_call(
        coarse_kernel(blocks),
        grid=(1,),
        in_specs=[SMEM] + [whole_block(b.shape) for b in (*targets, *launches)],
        out_specs=whole_block(shape),
        out_shape=jax.ShapeDtypeStruct(shape, jnp.float32),
        scratch_shapes=coarse_scratch(blocks, shape),
        name="coarse",
    )(place, *targets, *launches)


def final_kernel(blocks, chunks):
    def kernel(place, *refs):
        targets, launches = refs[:blocks], refs[blocks : 2 * blocks]
        refs = refs[2 * blocks :]
        fines, spread = refs[: len(chunks)], refs[len(chunks)]
        result, coef, ping, pong, wide = refs[len(chunks) + 1 :]
        rows = targets[0].shape[1]
        keep = jnp.where(place[1] > 0, 1.0, 0.0)
        planes = coarse_solve(targets, launches, coef, ping, pong, rows)
        height = planes[0].shape[0]
        stacked = jnp.concatenate(planes, axis=0) * keep
        spread_out = jnp.dot(
            stacked, spread[...], precision=lax.Precision.HIGHEST, preferred_element_type=jnp.float32
        )
        for i in range(len(planes)):
            part = spread_out[i * height : (i + 1) * height]
            tiles = part.shape[1] // LANES
            for at in range(tiles):
                piece = part[:, at * LANES : (at + 1) * LANES]
                wide[i * tiles + at, pl.ds(0, height, 2), :] = piece
                wide[i * tiles + at, pl.ds(1, height, 2), :] = piece
            field, row = i // rows, i % rows
            plane = jnp.concatenate([wide[i * tiles + at] for at in range(tiles)], axis=1)
            for chunk, fine in zip(chunks, fines):
                for at, which in enumerate(chunk):
                    for half in (0, 1):
                        result[which, field, 2 * row + half] = fine[at, field, 2 * row + half] + plane

    return kernel


def final_call(place, targets, launches, fines, chunks, out_shape):
    blocks = len(targets)
    block = targets[0].shape
    sz = out_shape[-1]
    spread = jnp.asarray(pool_matrix(sz).T.copy())
    return pl.pallas_call(
        final_kernel(blocks, chunks),
        grid=(1,),
        in_specs=[SMEM]
        + [whole_block(b.shape) for b in (*targets, *launches, *fines)]
        + [whole_block(spread.shape)],
        out_specs=whole_block(out_shape),
        out_shape=jax.ShapeDtypeStruct(out_shape, jnp.float32),
        scratch_shapes=coarse_scratch(blocks, block)
        + [pltpu.VMEM((2 * block[1] * sz // LANES, out_shape[-2], LANES), jnp.float32)],
        name="final",
    )(place, *targets, *launches, *fines, spread)


def local(slice_ends, initial, feed_rate, kill_rate):
    rows = feed_rate.shape[0]
    count = slice_ends.shape[0]
    quartets = lax.axis_size("tm")
    size = lax.axis_size("space")
    tm = lax.axis_index("tm")
    space = lax.axis_index("space")
    parity = (space % 2).astype(jnp.int32).reshape(1)
    place = jnp.stack([space, tm]).astype(jnp.int32)
    inner_pairs = [(i, i ^ 1) for i in range(size)]
    outer_pairs = [(i, (i + 1) % size if i % 2 else (i - 1) % size) for i in range(size)]

    def exchange(value):
        outer = lax.ppermute(value, "space", outer_pairs)
        inner = lax.ppermute(value, "space", inner_pairs)
        return value, inner, outer

    reach = -(-KC // (rows // 2))

    def to_next(value, distance):
        pairs = []
        for t in range(quartets - 1):
            for s in range(size):
                pairs.append((t * size + (s + distance) % size, (t + 1) * size + s))
        return lax.ppermute(value, ("tm", "space"), pairs)

    distances = range(-reach, reach + 1)
    width = min(rows, NF)

    coeffs = jnp.stack([feed_rate, kill_rate])[None]
    first_own = jnp.concatenate([coeffs] + [slice_ends[i - 1 : i] for i in CHUNKS[0]], axis=0)
    first = exchange(first_own)

    shifted = to_next(slice_ends[count - 1 : count], 0)
    start = jnp.where(tm == 0, initial[None], shifted)

    owns = [first_own]
    exchanged = [first]
    for chunk in CHUNKS[1:]:
        own = jnp.concatenate([start if i == 0 else slice_ends[i - 1 : i] for i in chunk], axis=0)
        owns.append(own)
        exchanged.append(exchange(own))

    early = early_call(slice_ends, feed_rate, kill_rate)
    launches = [to_next(early, d) for d in distances]

    rounds = NF // width
    fines = [None] * len(CHUNKS)
    target = None
    parts = exchanged
    for turn in range(rounds):
        following = []
        for at, chunk in enumerate(CHUNKS):
            with_coarse = turn == rounds - 1 and at == 0
            got = fine_call(parity, first, parts[at], len(chunk), width, with_coarse)
            fines[at] = got[0]
            if with_coarse:
                target = got[1]
            if turn < rounds - 1:
                following.append(exchange(got[0]))
        parts = following

    offset = jnp.zeros_like(target)
    for turn in range(quartets - 2):
        sent = target + offset
        offset = coarse_call(place, [to_next(sent, d) for d in distances], launches)
    sent = target if quartets <= 2 else target + offset
    targets = [to_next(sent, d) for d in distances]
    return final_call(place, targets, launches, fines, CHUNKS, slice_ends.shape)


def solution(mesh):
    in_specs = (
        P("tm", None, "space", None, None),
        P(None, "space", None, None),
        P("space", None, None),
        P("space", None, None),
    )
    out_specs = P("tm", None, "space", None, None)
    return jax.shard_map(local, mesh=mesh, in_specs=in_specs, out_specs=out_specs, check_vma=False)
```

time: 158 us -> 90 us (0.57)
  waiting for transfers between devices: 52.4 us -> 2 us
  local copies, waits for them, and re-layouts: 41.5 us -> 1.79 us
  starting transfers between devices: 37.5 us -> 62.2 us
  other arithmetic: 25 us -> 0.62 us
  Pallas kernels: 0 us -> 22 us
    ppermute x26 -> x31, waiting for transfers between devices: 52.4 us -> 2 us  [the longest x19 1.55 us: to_next(): return lax.ppermute(value, ('tm', 'space'), pairs)]
    ppermute x26 -> x31, starting transfers between devices: 37.5 us -> 62.2 us  [the longest x19 47.6 us: to_next(): return lax.ppermute(value, ('tm', 'space'), pairs)]
    pallas_call x0 -> x8, Pallas kernels: none -> 22 us  [the longest x6 17 us: fine_call(): pl.pallas_call(fine_kernel(n, rows, steps, with_coarse), grid=(1,), in_sp...]
    reshape x2 -> x0, local copies, waits for them, and re-layouts: 19.6 us -> none  [restrict(): values.reshape(leading + (sizes_x // 2, 2, sizes_y // 2, 2, sizes_z // 2,...]
    another operation x4 -> x0, local copies, waits for them, and re-layouts: 16.7 us -> none  [local(): coeffs = jnp.stack([feed_rate, kill_rate])[None]]
    reduce_sum x3 -> x0, other arithmetic: 8.1 us -> none  [restrict(): return jnp.mean(blocks, axis=(-5, -3, -1))]
    sub x25 -> x0, other arithmetic: 8.05 us -> none  [the longest x24 8.04 us: band_advance(): laplace_term = along_x + along_y + along_z - 6.0 * center]
    another operation x60 -> x1, other arithmetic: 5.24 us -> 0.56 us  [local(): place = jnp.stack([space, tm]).astype(jnp.int32)]
  transfers between devices with their start and end apart: 26 -> 31, of which waited for: 19 -> 2; matrix products, arithmetic and copies ran while one was open for 12% -> 1% of each run, Pallas kernels for 0% -> 19%
where the time goes in v1:
time: 90 us; the launch traced here: 89.3 us
  starting transfers between devices  62.2 us (69%)
  Pallas kernels  22 us (24%)
  waiting for transfers between devices  2 us (2%)
  local copies, waits for them, and re-layouts  1.79 us (2%)
    ppermute x19, starting transfers between devices, to_next(): return lax.ppermute(value, ('tm', 'space'), pairs)  47.6 us
    pallas_call x6, Pallas kernels, fine_call(): pl.pallas_call(fine_kernel(n, rows, steps, with_coarse), grid=(1,), in_sp...  17 us
    ppermute x6, starting transfers between devices, exchange(): outer = lax.ppermute(value, 'space', outer_pairs)  14.1 us
    pallas_call x1, Pallas kernels, final_call(): pl.pallas_call(final_kernel(blocks, chunks), grid=(1,), in_specs=[SMEM] +...  3.07 us
    pallas_call x1, Pallas kernels, early_call(): pl.pallas_call(early_kernel, grid=(1,), in_specs=[whole_block(feed_rate.s...  1.91 us
  transfers between devices with their start and end apart: 31, of which 2 were waited for; matrix products, arithmetic and copies ran while one was open for 1% of the time, Pallas kernels for 19%

profile of v1, /device:TPU:0, one launch (start us, length us, event | category | flops | bytes accessed | tf_op | source)
XLA Modules:
  0.0 89.3 jit_solution(4958185555065422624)
XLA Ops:
  0.0 1.9 %early.1 = f32[4,2,8,128]{3,2,1,0:T(8,128)} custom-call(f32[4,16,256]{2,1,0:T(8,128)} %feed.1, f32[4,16,256]{2,1,0:T(8,128)} %kill.1, f32[4,2,4,16,256]{4,3,2,1,0:T(8,128)} %last.1, f32[256,128]{1,0:T(8,128)} %constant.27.clone.refs_6_.pool), custom_call_target="tpu_custom_call" | custom-call | tf_op jit(solution)/shard_map/early/pallas_call | solution.py:194
  1.9 6.0 %collective-permute-start.13 = (f32[4,2,8,128]{3,2,1,0:T(8,128)}, f32[4,2,8,128]{3,2,1,0:T(8,128)S(1)}, u32[]{:S(2)}, u32[]{:S(2)}) collective-permute-start(f32[4,2,8,128]{3,2,1,0:T(8,128)} %early.1), channel_id=1, source_target_pairs={{12,16},{13,17},{14,18},{15,19},{0,20},{1,21},{2,22},{3,23},{4,24}... | collective-permute-start | bytes 98312 | tf_op jit(solution)/shard_map/ppermute | solution.py:343
  7.9 1.3 %collective-permute-start.14 = (f32[4,2,8,128]{3,2,1,0:T(8,128)}, f32[4,2,8,128]{3,2,1,0:T(8,128)S(1)}, u32[]{:S(2)}, u32[]{:S(2)}) collective-permute-start(f32[4,2,8,128]{3,2,1,0:T(8,128)} %early.1), channel_id=1, source_target_pairs={{13,16},{14,17},{15,18},{0,19},{1,20},{2,21},{3,22},{4,23},{5,24},... | collective-permute-start | bytes 98312 | tf_op jit(solution)/shard_map/ppermute | solution.py:343
  9.2 1.3 %collective-permute-start.15 = (f32[4,2,8,128]{3,2,1,0:T(8,128)}, f32[4,2,8,128]{3,2,1,0:T(8,128)S(1)}, u32[]{:S(2)}, u32[]{:S(2)}) collective-permute-start(f32[4,2,8,128]{3,2,1,0:T(8,128)} %early.1), channel_id=1, source_target_pairs={{14,16},{15,17},{0,18},{1,19},{2,20},{3,21},{4,22},{5,23},{6,24},{... | collective-permute-start | bytes 98312 | tf_op jit(solution)/shard_map/ppermute | solution.py:343
  10.5 1.3 %collective-permute-start.16 = (f32[4,2,8,128]{3,2,1,0:T(8,128)}, f32[4,2,8,128]{3,2,1,0:T(8,128)S(1)}, u32[]{:S(2)}, u32[]{:S(2)}) collective-permute-start(f32[4,2,8,128]{3,2,1,0:T(8,128)} %early.1), channel_id=1, source_target_pairs={{15,16},{0,17},{1,18},{2,19},{3,20},{4,21},{5,22},{6,23},{7,24},{8... | collective-permute-start | bytes 98312 | tf_op jit(solution)/shard_map/ppermute | solution.py:343
  11.9 1.3 %collective-permute-start.26 = (f32[1,2,4,16,256]{4,3,2,1,0:T(8,128)S(1)}, f32[1,2,4,16,256]{4,3,2,1,0:T(8,128)S(1)}, u32[]{:S(2)}, u32[]{:S(2)}) collective-permute-start(f32[1,2,4,16,256]{4,3,2,1,0:T(8,128)S(1)} %get-tuple-element.9), channel_id=1, source_target_pairs={{0,16},{1,17},{2,18},{3,19},{4,20},{5,21},{6,22},{7,23},{8,24},{9,... | collective-permute-start | bytes 393224 | tf_op jit(solution)/shard_map/ppermute | solution.py:343
  13.3 0.0 copy-start
  13.3 0.0 collective-permute-done.13.refs_9_
  13.3 0.2 collective-permute-start
  13.5 0.4 copy-done.20
  13.9 0.0 collective-permute-done.14.refs_10_
  13.9 0.0 copy-done
  14.0 3.2 %collective-permute-start.1 = (f32[2,2,4,16,256]{4,3,2,1,0:T(8,128)S(1)}, f32[2,2,4,16,256]{4,3,2,1,0:T(8,128)S(1)}, u32[]{:S(2)}, u32[]{:S(2)}) collective-permute-start(f32[2,2,4,16,256]{4,3,2,1,0:T(8,128)S(1)} %pad_maximum_fusion.refs_0_.refs_3_), channel_id=1, source_target_pairs={{0,15},{1,2},{2,1},{3,4},{4,3},{5,6},{6,5},{7,8},{8,7},{9,10},{10,... | collective-permute-start | bytes 786440 | tf_op jit(solution)/shard_map/ppermute | solution.py:332
  17.2 0.0 collective-permute-done.15.refs_11_
  17.2 0.0 collective-permute-start.22
  17.2 0.0 collective-permute-done.16.refs_12_
  17.2 1.7 %collective-permute-start.23 = (f32[2,2,4,16,256]{4,3,2,1,0:T(8,128)S(1)}, f32[2,2,4,16,256]{4,3,2,1,0:T(8,128)S(1)}, u32[]{:S(2)}, u32[]{:S(2)}) collective-permute-start(f32[2,2,4,16,256]{4,3,2,1,0:T(8,128)S(1)} %pad_maximum_fusion.1.refs_3_), channel_id=1, source_target_pairs={{0,15},{1,2},{2,1},{3,4},{4,3},{5,6},{6,5},{7,8},{8,7},{9,10},{10,... | collective-permute-start | bytes 786440 | tf_op jit(solution)/shard_map/ppermute | solution.py:332
  18.9 2.6 %collective-permute-start.17 = (f32[4,2,8,128]{3,2,1,0:T(8,128)S(1)}, f32[4,2,8,128]{3,2,1,0:T(8,128)S(1)}, u32[]{:S(2)}, u32[]{:S(2)}) collective-permute-start(f32[4,2,8,128]{3,2,1,0:T(8,128)S(1)} %copy-done.26), channel_id=1, source_target_pairs={{0,16},{1,17},{2,18},{3,19},{4,20},{5,21},{6,22},{7,23},{8,24},{9,... | collective-permute-start | bytes 98312 | tf_op jit(solution)/shard_map/ppermute | solution.py:343
  21.5 1.5 %collective-permute-done.17.refs_13_ = f32[4,2,8,128]{3,2,1,0:T(8,128)S(1)} collective-permute-done((f32[4,2,8,128]{3,2,1,0:T(8,128)S(1)}, f32[4,2,8,128]{3,2,1,0:T(8,128)S(1)}, u32[]{:S(2)}, u32[]{:S(2)}) %collective-permute-start.17) | collective-permute-done | bytes 32800 | tf_op jit(solution)/shard_map/ppermute | solution.py:343
  23.0 3.2 %collective-permute-start.28 = (f32[1,2,4,16,256]{4,3,2,1,0:T(8,128)S(1)}, f32[1,2,4,16,256]{4,3,2,1,0:T(8,128)S(1)}, u32[]{:S(2)}, u32[]{:S(2)}) collective-permute-start(f32[1,2,4,16,256]{4,3,2,1,0:T(8,128)S(1)} %bitcast_select_fusion.refs_3_), channel_id=1, source_target_pairs={{0,15},{1,2},{2,1},{3,4},{4,3},{5,6},{6,5},{7,8},{8,7},{9,10},{10,... | collective-permute-start | bytes 393224 | tf_op jit(solution)/shard_map/ppermute | solution.py:332
  26.2 0.0 collective-permute-done.1.refs_2_.refs_5_
  26.2 5.0 %collective-permute-start.18 = (f32[4,2,8,128]{3,2,1,0:T(8,128)S(1)}, f32[4,2,8,128]{3,2,1,0:T(8,128)S(1)}, u32[]{:S(2)}, u32[]{:S(2)}) collective-permute-start(f32[4,2,8,128]{3,2,1,0:T(8,128)S(1)} %copy-done.26), channel_id=1, source_target_pairs={{1,16},{2,17},{3,18},{4,19},{5,20},{6,21},{7,22},{8,23},{9,24},{10... | collective-permute-start | bytes 98312 | tf_op jit(solution)/shard_map/ppermute | solution.py:343
  31.2 1.3 %collective-permute-start.19 = (f32[4,2,8,128]{3,2,1,0:T(8,128)S(1)}, f32[4,2,8,128]{3,2,1,0:T(8,128)S(1)}, u32[]{:S(2)}, u32[]{:S(2)}) collective-permute-start(f32[4,2,8,128]{3,2,1,0:T(8,128)S(1)} %copy-done.26), channel_id=1, source_target_pairs={{2,16},{3,17},{4,18},{5,19},{6,20},{7,21},{8,22},{9,23},{10,24},{1... | collective-permute-start | bytes 98312 | tf_op jit(solution)/shard_map/ppermute | solution.py:343
  32.6 2.6 %fine.6.refs_3_ = f32[1,2,4,16,256]{4,3,2,1,0:T(8,128)} custom-call(s32[1]{0:T(128)} %bitcast.2.parity, f32[2,2,4,16,256]{4,3,2,1,0:T(8,128)} %copy-done, f32[2,2,4,16,256]{4,3,2,1,0:T(8,128)} %copy-done.1, f32[2,2,4,16,256]{4,3,2,1,0:T(8,128)} %copy-done.2, f32[2,2,4,16,256]{4,3,2,1,0:T(8,128)} %copy-done, f32[2,2,4,16,256]{4,3,2,1,0:T(8,128)} %copy-done.1, ...), custom_call_target="tpu_custom_call" | custom-call | tf_op jit(solution)/shard_map/fine/pallas_call | solution.py:167
  35.2 0.0 collective-permute-done.23.refs_5_
  35.3 0.1 collective-permute-start.2
  35.4 0.6 copy-done.12
  36.0 3.3 %fine.8.refs_3_ = f32[2,2,4,16,256]{4,3,2,1,0:T(8,128)} custom-call(s32[1]{0:T(128)} %bitcast.2.parity, f32[2,2,4,16,256]{4,3,2,1,0:T(8,128)} %copy-done, f32[2,2,4,16,256]{4,3,2,1,0:T(8,128)} %copy-done.1, f32[2,2,4,16,256]{4,3,2,1,0:T(8,128)} %copy-done.2, f32[2,2,4,16,256]{4,3,2,1,0:T(8,128)} %copy-done.4, f32[2,2,4,16,256]{4,3,2,1,0:T(8,128)} %copy-done.11, ...), custom_call_target="tpu_custom_call" | custom-call | tf_op jit(solution)/shard_map/fine/pallas_call | solution.py:167
  39.3 0.0 collective-permute-done.18.refs_14_
  39.3 0.1 collective-permute-start.24
  39.3 1.5 %collective-permute-start.25 = (f32[2,2,4,16,256]{4,3,2,1,0:T(8,128)}, f32[2,2,4,16,256]{4,3,2,1,0:T(8,128)S(1)}, u32[]{:S(2)}, u32[]{:S(2)}) collective-permute-start(f32[2,2,4,16,256]{4,3,2,1,0:T(8,128)} %fine.8.refs_3_), channel_id=1, source_target_pairs={{0,15},{1,2},{2,1},{3,4},{4,3},{5,6},{6,5},{7,8},{8,7},{9,10},{10,... | collective-permute-start | bytes 786440 | tf_op jit(solution)/shard_map/ppermute | solution.py:332
  40.8 3.0 %collective-permute-start.3 = (f32[1,2,4,16,256]{4,3,2,1,0:T(8,128)S(1)}, f32[1,2,4,16,256]{4,3,2,1,0:T(8,128)S(1)}, u32[]{:S(2)}, u32[]{:S(2)}) collective-permute-start(f32[1,2,4,16,256]{4,3,2,1,0:T(8,128)S(1)} %copy-done.5), channel_id=1, source_target_pairs={{0,15},{1,2},{2,1},{3,4},{4,3},{5,6},{6,5},{7,8},{8,7},{9,10},{10,... | collective-permute-start | bytes 393224 | tf_op jit(solution)/shard_map/ppermute | solution.py:332
  43.9 0.0 collective-permute-done.28.refs_5_
  43.9 1.3 %collective-permute-start.20 = (f32[4,2,8,128]{3,2,1,0:T(8,128)S(1)}, f32[4,2,8,128]{3,2,1,0:T(8,128)S(1)}, u32[]{:S(2)}, u32[]{:S(2)}) collective-permute-start(f32[4,2,8,128]{3,2,1,0:T(8,128)S(1)} %copy-done.26), channel_id=1, source_target_pairs={{3,16},{4,17},{5,18},{6,19},{7,20},{8,21},{9,22},{10,23},{11,24},{... | collective-permute-start | bytes 98312 | tf_op jit(solution)/shard_map/ppermute | solution.py:343
  45.2 2.5 %fine.10.refs_3_ = f32[1,2,4,16,256]{4,3,2,1,0:T(8,128)} custom-call(s32[1]{0:T(128)} %bitcast.2.parity, f32[2,2,4,16,256]{4,3,2,1,0:T(8,128)} %copy-done, f32[2,2,4,16,256]{4,3,2,1,0:T(8,128)} %copy-done.1, f32[2,2,4,16,256]{4,3,2,1,0:T(8,128)} %copy-done.2, f32[1,2,4,16,256]{4,3,2,1,0:T(8,128)} %copy-done.6, f32[1,2,4,16,256]{4,3,2,1,0:T(8,128)} %copy-done.13, ...), custom_call_target="tpu_custom_call" | custom-call | tf_op jit(solution)/shard_map/fine/pallas_call | solution.py:167
  47.7 0.0 collective-permute-done.20.refs_16_
  47.7 0.1 collective-permute-start.29
  47.8 0.0 collective-permute-done.2.refs_4_
  47.8 1.5 %collective-permute-start.30 = (f32[1,2,4,16,256]{4,3,2,1,0:T(8,128)}, f32[1,2,4,16,256]{4,3,2,1,0:T(8,128)S(1)}, u32[]{:S(2)}, u32[]{:S(2)}) collective-permute-start(f32[1,2,4,16,256]{4,3,2,1,0:T(8,128)} %fine.10.refs_3_), channel_id=1, source_target_pairs={{0,15},{1,2},{2,1},{3,4},{4,3},{5,6},{6,5},{7,8},{8,7},{9,10},{10,... | collective-permute-start | bytes 393224 | tf_op jit(solution)/shard_map/ppermute | solution.py:332
  49.4 0.4 collective-permute-done.3.refs_5_
  49.8 4.2 %collective-permute-start.21 = (f32[4,2,8,128]{3,2,1,0:T(8,128)S(1)}, f32[4,2,8,128]{3,2,1,0:T(8,128)S(1)}, u32[]{:S(2)}, u32[]{:S(2)}) collective-permute-start(f32[4,2,8,128]{3,2,1,0:T(8,128)S(1)} %copy-done.26), channel_id=1, source_target_pairs={{4,16},{5,17},{6,18},{7,19},{8,20},{9,21},{10,22},{11,23},{12,24},... | collective-permute-start | bytes 98312 | tf_op jit(solution)/shard_map/ppermute | solution.py:343
  54.1 2.7 %fine.7 = (f32[1,2,4,16,256]{4,3,2,1,0:T(8,128)}, f32[2,2,8,128]{3,2,1,0:T(8,128)}) custom-call(s32[1]{0:T(128)} %bitcast.2.parity, f32[2,2,4,16,256]{4,3,2,1,0:T(8,128)} %copy-done, f32[2,2,4,16,256]{4,3,2,1,0:T(8,128)} %copy-done.1, f32[2,2,4,16,256]{4,3,2,1,0:T(8,128)} %copy-done.2, f32[1,2,4,16,256]{4,3,2,1,0:T(8,128)} %fine.6.refs_3_, ...), custom_call_target="tpu_custom_call" | custom-call | tf_op jit(solution)/shard_map/fine/pallas_call | solution.py:167
  56.8 6.8 %collective-permute-start.10 = (f32[2,2,8,128]{3,2,1,0:T(8,128)}, f32[2,2,8,128]{3,2,1,0:T(8,128)S(1)}, u32[]{:S(2)}, u32[]{:S(2)}) collective-permute-start(f32[2,2,8,128]{3,2,1,0:T(8,128)} %get-tuple-element.7), channel_id=1, source_target_pairs={{2,16},{3,17},{4,18},{5,19},{6,20},{7,21},{8,22},{9,23},{10,24},{1... | collective-permute-start | bytes 49160 | tf_op jit(solution)/shard_map/ppermute | solution.py:343
  63.7 1.3 %collective-permute-start.11 = (f32[2,2,8,128]{3,2,1,0:T(8,128)}, f32[2,2,8,128]{3,2,1,0:T(8,128)S(1)}, u32[]{:S(2)}, u32[]{:S(2)}) collective-permute-start(f32[2,2,8,128]{3,2,1,0:T(8,128)} %get-tuple-element.7), channel_id=1, source_target_pairs={{3,16},{4,17},{5,18},{6,19},{7,20},{8,21},{9,22},{10,23},{11,24},{... | collective-permute-start | bytes 49160 | tf_op jit(solution)/shard_map/ppermute | solution.py:343
  65.0 1.3 %collective-permute-start.12 = (f32[2,2,8,128]{3,2,1,0:T(8,128)}, f32[2,2,8,128]{3,2,1,0:T(8,128)S(1)}, u32[]{:S(2)}, u32[]{:S(2)}) collective-permute-start(f32[2,2,8,128]{3,2,1,0:T(8,128)} %get-tuple-element.7), channel_id=1, source_target_pairs={{4,16},{5,17},{6,18},{7,19},{8,20},{9,21},{10,22},{11,23},{12,24},... | collective-permute-start | bytes 49160 | tf_op jit(solution)/shard_map/ppermute | solution.py:343
  66.3 1.3 %collective-permute-start.4 = (f32[2,2,8,128]{3,2,1,0:T(8,128)}, f32[2,2,8,128]{3,2,1,0:T(8,128)S(1)}, u32[]{:S(2)}, u32[]{:S(2)}) collective-permute-start(f32[2,2,8,128]{3,2,1,0:T(8,128)} %get-tuple-element.7), channel_id=1, source_target_pairs={{12,16},{13,17},{14,18},{15,19},{0,20},{1,21},{2,22},{3,23},{4,24}... | collective-permute-start | bytes 49160 | tf_op jit(solution)/shard_map/ppermute | solution.py:343
  67.6 1.3 %collective-permute-start.5 = (f32[2,2,8,128]{3,2,1,0:T(8,128)}, f32[2,2,8,128]{3,2,1,0:T(8,128)S(1)}, u32[]{:S(2)}, u32[]{:S(2)}) collective-permute-start(f32[2,2,8,128]{3,2,1,0:T(8,128)} %get-tuple-element.7), channel_id=1, source_target_pairs={{13,16},{14,17},{15,18},{0,19},{1,20},{2,21},{3,22},{4,23},{5,24},... | collective-permute-start | bytes 49160 | tf_op jit(solution)/shard_map/ppermute | solution.py:343
  68.9 1.3 %collective-permute-start.6 = (f32[2,2,8,128]{3,2,1,0:T(8,128)}, f32[2,2,8,128]{3,2,1,0:T(8,128)S(1)}, u32[]{:S(2)}, u32[]{:S(2)}) collective-permute-start(f32[2,2,8,128]{3,2,1,0:T(8,128)} %get-tuple-element.7), channel_id=1, source_target_pairs={{14,16},{15,17},{0,18},{1,19},{2,20},{3,21},{4,22},{5,23},{6,24},{... | collective-permute-start | bytes 49160 | tf_op jit(solution)/shard_map/ppermute | solution.py:343
  70.3 1.3 %collective-permute-start.7 = (f32[2,2,8,128]{3,2,1,0:T(8,128)}, f32[2,2,8,128]{3,2,1,0:T(8,128)S(1)}, u32[]{:S(2)}, u32[]{:S(2)}) collective-permute-start(f32[2,2,8,128]{3,2,1,0:T(8,128)} %get-tuple-element.7), channel_id=1, source_target_pairs={{15,16},{0,17},{1,18},{2,19},{3,20},{4,21},{5,22},{6,23},{7,24},{8... | collective-permute-start | bytes 49160 | tf_op jit(solution)/shard_map/ppermute | solution.py:343
  71.6 5.6 %collective-permute-start.8 = (f32[2,2,8,128]{3,2,1,0:T(8,128)}, f32[2,2,8,128]{3,2,1,0:T(8,128)S(1)}, u32[]{:S(2)}, u32[]{:S(2)}) collective-permute-start(f32[2,2,8,128]{3,2,1,0:T(8,128)} %get-tuple-element.7), channel_id=1, source_target_pairs={{0,16},{1,17},{2,18},{3,19},{4,20},{5,21},{6,22},{7,23},{8,24},{9,... | collective-permute-start | bytes 49160 | tf_op jit(solution)/shard_map/ppermute | solution.py:343
  77.1 0.0 collective-permute-done.25.refs_5_
  77.2 1.9 %collective-permute-start.9 = (f32[2,2,8,128]{3,2,1,0:T(8,128)}, f32[2,2,8,128]{3,2,1,0:T(8,128)S(1)}, u32[]{:S(2)}, u32[]{:S(2)}) collective-permute-start(f32[2,2,8,128]{3,2,1,0:T(8,128)} %get-tuple-element.7), channel_id=1, source_target_pairs={{1,16},{2,17},{3,18},{4,19},{5,20},{6,21},{7,22},{8,23},{9,24},{10... | collective-permute-start | bytes 49160 | tf_op jit(solution)/shard_map/ppermute | solution.py:343
  79.1 0.6 pad_add_fusion.place
  79.6 2.5 %fine.11.refs_20_ = f32[1,2,4,16,256]{4,3,2,1,0:T(8,128)} custom-call(s32[1]{0:T(128)} %bitcast.2.parity, f32[2,2,4,16,256]{4,3,2,1,0:T(8,128)} %copy-done, f32[2,2,4,16,256]{4,3,2,1,0:T(8,128)} %copy-done.1, f32[2,2,4,16,256]{4,3,2,1,0:T(8,128)} %copy-done.2, f32[1,2,4,16,256]{4,3,2,1,0:T(8,128)} %fine.10.refs_3_, f32[1,2,4,16,256]{4,3,2,1,0:T(8,128)} %copy-done.14, ...), custom_call_target="tpu_custom_call" | custom-call | tf_op jit(solution)/shard_map/fine/pallas_call | solution.py:167
  82.2 3.3 %fine.9.refs_19_ = f32[2,2,4,16,256]{4,3,2,1,0:T(8,128)} custom-call(s32[1]{0:T(128)} %bitcast.2.parity, f32[2,2,4,16,256]{4,3,2,1,0:T(8,128)} %copy-done, f32[2,2,4,16,256]{4,3,2,1,0:T(8,128)} %copy-done.1, f32[2,2,4,16,256]{4,3,2,1,0:T(8,128)} %copy-done.2, f32[2,2,4,16,256]{4,3,2,1,0:T(8,128)} %fine.8.refs_3_, f32[2,2,4,16,256]{4,3,2,1,0:T(8,128)} %copy-done.9, ...), custom_call_target="tpu_custom_call" | custom-call | tf_op jit(solution)/shard_map/fine/pallas_call | solution.py:167
  85.5 0.0 collective-permute-done.5.refs_1_
  85.6 0.0 collective-permute-done.7.refs_3_
  85.6 0.0 collective-permute-done.8.refs_4_
  85.6 0.5 copy-done.34
  86.1 0.0 copy-done.35
  86.1 0.0 copy-done.36
  86.2 0.0 copy-done.37
  86.2 0.0 copy-done.38
  86.2 3.1 %final.1 = f32[4,2,4,16,256]{4,3,2,1,0:T(8,128)} custom-call(s32[2]{0:T(128)} %pad_add_fusion.place, f32[2,2,8,128]{3,2,1,0:T(8,128)} %copy-done.33, f32[2,2,8,128]{3,2,1,0:T(8,128)} %copy-done.34, f32[2,2,8,128]{3,2,1,0:T(8,128)} %copy-done.35, f32[2,2,8,128]{3,2,1,0:T(8,128)} %copy-done.36, f32[2,2,8,128]{3,2,1,0:T(8,128)} %copy-done.37, ...), custom_call_target="tpu_custom_call" | custom-call | tf_op jit(solution)/shard_map/final/pallas_call | solution.py:305
  (90 shorter events, 0.3 us)
Async XLA Ops:
  0.0 11.8 %copy-start.3 = (f32[4,2,4,16,256]{4,3,2,1,0:T(8,128)S(1)}, f32[4,2,4,16,256]{4,3,2,1,0:T(8,128)}, u32[]{:S(2)}) copy-start(f32[4,2,4,16,256]{4,3,2,1,0:T(8,128)} %last.1) | copy-start | bytes 1572868
  1.9 11.3 %copy-start.7 = (f32[4,16,256]{2,1,0:T(8,128)S(1)}, f32[4,16,256]{2,1,0:T(8,128)}, u32[]{:S(2)}) copy-start(f32[4,16,256]{2,1,0:T(8,128)} %kill.1) | copy-start | bytes 196612
  1.9 11.3 %copy-start.8 = (f32[4,16,256]{2,1,0:T(8,128)S(1)}, f32[4,16,256]{2,1,0:T(8,128)}, u32[]{:S(2)}) copy-start(f32[4,16,256]{2,1,0:T(8,128)} %feed.1) | copy-start | bytes 196612
  1.9 11.4 %collective-permute-start.13 = (f32[4,2,8,128]{3,2,1,0:T(8,128)}, f32[4,2,8,128]{3,2,1,0:T(8,128)S(1)}, u32[]{:S(2)}, u32[]{:S(2)}) collective-permute-start(f32[4,2,8,128]{3,2,1,0:T(8,128)} %early.1), channel_id=1, source_target_pairs={{12,16},{13,17},{14,18},{15,19},{0,20},{1,21},{2,22},{3,23},{4,24}... | collective-permute-start | bytes 98312 | tf_op jit(solution)/shard_map/ppermute | solution.py:343
  7.9 6.0 %collective-permute-start.14 = (f32[4,2,8,128]{3,2,1,0:T(8,128)}, f32[4,2,8,128]{3,2,1,0:T(8,128)S(1)}, u32[]{:S(2)}, u32[]{:S(2)}) collective-permute-start(f32[4,2,8,128]{3,2,1,0:T(8,128)} %early.1), channel_id=1, source_target_pairs={{13,16},{14,17},{15,18},{0,19},{1,20},{2,21},{3,22},{4,23},{5,24},... | collective-permute-start | bytes 98312 | tf_op jit(solution)/shard_map/ppermute | solution.py:343
  9.2 7.9 %collective-permute-start.15 = (f32[4,2,8,128]{3,2,1,0:T(8,128)}, f32[4,2,8,128]{3,2,1,0:T(8,128)S(1)}, u32[]{:S(2)}, u32[]{:S(2)}) collective-permute-start(f32[4,2,8,128]{3,2,1,0:T(8,128)} %early.1), channel_id=1, source_target_pairs={{14,16},{15,17},{0,18},{1,19},{2,20},{3,21},{4,22},{5,23},{6,24},{... | collective-permute-start | bytes 98312 | tf_op jit(solution)/shard_map/ppermute | solution.py:343
  10.5 6.7 %collective-permute-start.16 = (f32[4,2,8,128]{3,2,1,0:T(8,128)}, f32[4,2,8,128]{3,2,1,0:T(8,128)S(1)}, u32[]{:S(2)}, u32[]{:S(2)}) collective-permute-start(f32[4,2,8,128]{3,2,1,0:T(8,128)} %early.1), channel_id=1, source_target_pairs={{15,16},{0,17},{1,18},{2,19},{3,20},{4,21},{5,22},{6,23},{7,24},{8... | collective-permute-start | bytes 98312 | tf_op jit(solution)/shard_map/ppermute | solution.py:343
  11.9 7.0 %collective-permute-start.26 = (f32[1,2,4,16,256]{4,3,2,1,0:T(8,128)S(1)}, f32[1,2,4,16,256]{4,3,2,1,0:T(8,128)S(1)}, u32[]{:S(2)}, u32[]{:S(2)}) collective-permute-start(f32[1,2,4,16,256]{4,3,2,1,0:T(8,128)S(1)} %get-tuple-element.9), channel_id=1, source_target_pairs={{0,16},{1,17},{2,18},{3,19},{4,20},{5,21},{6,22},{7,23},{8,24},{9,... | collective-permute-start | bytes 393224 | tf_op jit(solution)/shard_map/ppermute | solution.py:343
  13.3 0.7 copy-start
  13.3 9.7 %collective-permute-start = (f32[2,2,4,16,256]{4,3,2,1,0:T(8,128)S(1)}, f32[2,2,4,16,256]{4,3,2,1,0:T(8,128)S(1)}, u32[]{:S(2)}, u32[]{:S(2)}) collective-permute-start(f32[2,2,4,16,256]{4,3,2,1,0:T(8,128)S(1)} %pad_maximum_fusion.refs_0_.refs_3_), channel_id=1, source_target_pairs={{0,1},{1,0},{2,3},{3,2},{4,5},{5,4},{6,7},{7,6},{8,9},{9,8},{10,11... | collective-permute-start | bytes 786440 | tf_op jit(solution)/shard_map/ppermute | solution.py:333
  13.5 5.4 %copy-start.26 = (f32[4,2,8,128]{3,2,1,0:T(8,128)S(1)}, f32[4,2,8,128]{3,2,1,0:T(8,128)}, u32[]{:S(2)}) copy-start(f32[4,2,8,128]{3,2,1,0:T(8,128)} %early.1) | copy-start | bytes 98308
  13.5 8.0 %copy-start.19 = (f32[2,4,16,256]{3,2,1,0:T(8,128)S(1)}, f32[2,4,16,256]{3,2,1,0:T(8,128)}, u32[]{:S(2)}) copy-start(f32[2,4,16,256]{3,2,1,0:T(8,128)} %param.8) | copy-start | bytes 393220
  13.9 21.3 %copy-start.4 = (f32[2,2,4,16,256]{4,3,2,1,0:T(8,128)}, f32[2,2,4,16,256]{4,3,2,1,0:T(8,128)S(1)}, u32[]{:S(2)}) copy-start(f32[2,2,4,16,256]{4,3,2,1,0:T(8,128)S(1)} %pad_maximum_fusion.1.refs_3_) | copy-start | bytes 786436
  14.0 7.5 %copy-start.21 = (f32[4,2,8,128]{3,2,1,0:T(8,128)}, f32[4,2,8,128]{3,2,1,0:T(8,128)S(1)}, u32[]{:S(2)}) copy-start(f32[4,2,8,128]{3,2,1,0:T(8,128)S(1)} %collective-permute-done.14.refs_10_) | copy-start | bytes 98308
  14.0 12.2 %collective-permute-start.1 = (f32[2,2,4,16,256]{4,3,2,1,0:T(8,128)S(1)}, f32[2,2,4,16,256]{4,3,2,1,0:T(8,128)S(1)}, u32[]{:S(2)}, u32[]{:S(2)}) collective-permute-start(f32[2,2,4,16,256]{4,3,2,1,0:T(8,128)S(1)} %pad_maximum_fusion.refs_0_.refs_3_), channel_id=1, source_target_pairs={{0,15},{1,2},{2,1},{3,4},{4,3},{5,6},{6,5},{7,8},{8,7},{9,10},{10,... | collective-permute-start | bytes 786440 | tf_op jit(solution)/shard_map/ppermute | solution.py:332
  17.2 4.3 %copy-start.22 = (f32[4,2,8,128]{3,2,1,0:T(8,128)}, f32[4,2,8,128]{3,2,1,0:T(8,128)S(1)}, u32[]{:S(2)}) copy-start(f32[4,2,8,128]{3,2,1,0:T(8,128)S(1)} %collective-permute-done.15.refs_11_) | copy-start | bytes 98308
  17.2 14.0 %collective-permute-start.22 = (f32[2,2,4,16,256]{4,3,2,1,0:T(8,128)S(1)}, f32[2,2,4,16,256]{4,3,2,1,0:T(8,128)S(1)}, u32[]{:S(2)}, u32[]{:S(2)}) collective-permute-start(f32[2,2,4,16,256]{4,3,2,1,0:T(8,128)S(1)} %pad_maximum_fusion.1.refs_3_), channel_id=1, source_target_pairs={{0,1},{1,0},{2,3},{3,2},{4,5},{5,4},{6,7},{7,6},{8,9},{9,8},{10,11... | collective-permute-start | bytes 786440 | tf_op jit(solution)/shard_map/ppermute | solution.py:333
  17.2 4.3 %copy-start.23 = (f32[4,2,8,128]{3,2,1,0:T(8,128)}, f32[4,2,8,128]{3,2,1,0:T(8,128)S(1)}, u32[]{:S(2)}) copy-start(f32[4,2,8,128]{3,2,1,0:T(8,128)S(1)} %collective-permute-done.16.refs_12_) | copy-start | bytes 98308
  17.2 18.0 %collective-permute-start.23 = (f32[2,2,4,16,256]{4,3,2,1,0:T(8,128)S(1)}, f32[2,2,4,16,256]{4,3,2,1,0:T(8,128)S(1)}, u32[]{:S(2)}, u32[]{:S(2)}) collective-permute-start(f32[2,2,4,16,256]{4,3,2,1,0:T(8,128)S(1)} %pad_maximum_fusion.1.refs_3_), channel_id=1, source_target_pairs={{0,15},{1,2},{2,1},{3,4},{4,3},{5,6},{6,5},{7,8},{8,7},{9,10},{10,... | collective-permute-start | bytes 786440 | tf_op jit(solution)/shard_map/ppermute | solution.py:332
  18.9 4.1 %collective-permute-start.17 = (f32[4,2,8,128]{3,2,1,0:T(8,128)S(1)}, f32[4,2,8,128]{3,2,1,0:T(8,128)S(1)}, u32[]{:S(2)}, u32[]{:S(2)}) collective-permute-start(f32[4,2,8,128]{3,2,1,0:T(8,128)S(1)} %copy-done.26), channel_id=1, source_target_pairs={{0,16},{1,17},{2,18},{3,19},{4,20},{5,21},{6,22},{7,23},{8,24},{9,... | collective-permute-start | bytes 98312 | tf_op jit(solution)/shard_map/ppermute | solution.py:343
  21.5 13.7 %copy-start.6 = (f32[1,2,4,16,256]{4,3,2,1,0:T(8,128)}, f32[1,2,4,16,256]{4,3,2,1,0:T(8,128)S(1)}, u32[]{:S(2)}) copy-start(f32[1,2,4,16,256]{4,3,2,1,0:T(8,128)S(1)} %bitcast_select_fusion.refs_3_) | copy-start | bytes 393220
  23.0 12.2 %copy-start.24 = (f32[4,2,8,128]{3,2,1,0:T(8,128)}, f32[4,2,8,128]{3,2,1,0:T(8,128)S(1)}, u32[]{:S(2)}) copy-start(f32[4,2,8,128]{3,2,1,0:T(8,128)S(1)} %collective-permute-done.17.refs_13_) | copy-start | bytes 98308
  23.0 17.8 %collective-permute-start.27 = (f32[1,2,4,16,256]{4,3,2,1,0:T(8,128)S(1)}, f32[1,2,4,16,256]{4,3,2,1,0:T(8,128)S(1)}, u32[]{:S(2)}, u32[]{:S(2)}) collective-permute-start(f32[1,2,4,16,256]{4,3,2,1,0:T(8,128)S(1)} %bitcast_select_fusion.refs_3_), channel_id=1, source_target_pairs={{0,1},{1,0},{2,3},{3,2},{4,5},{5,4},{6,7},{7,6},{8,9},{9,8},{10,11... | collective-permute-start | bytes 393224 | tf_op jit(solution)/shard_map/ppermute | solution.py:333
  23.0 9.5 %copy-start.1 = (f32[2,2,4,16,256]{4,3,2,1,0:T(8,128)}, f32[2,2,4,16,256]{4,3,2,1,0:T(8,128)S(1)}, u32[]{:S(2)}) copy-start(f32[2,2,4,16,256]{4,3,2,1,0:T(8,128)S(1)} %collective-permute-done.refs_1_.refs_4_) | copy-start | bytes 786436
  23.0 20.8 %collective-permute-start.28 = (f32[1,2,4,16,256]{4,3,2,1,0:T(8,128)S(1)}, f32[1,2,4,16,256]{4,3,2,1,0:T(8,128)S(1)}, u32[]{:S(2)}, u32[]{:S(2)}) collective-permute-start(f32[1,2,4,16,256]{4,3,2,1,0:T(8,128)S(1)} %bitcast_select_fusion.refs_3_), channel_id=1, source_target_pairs={{0,15},{1,2},{2,1},{3,4},{4,3},{5,6},{6,5},{7,8},{8,7},{9,10},{10,... | collective-permute-start | bytes 393224 | tf_op jit(solution)/shard_map/ppermute | solution.py:332
  26.2 6.4 %copy-start.2 = (f32[2,2,4,16,256]{4,3,2,1,0:T(8,128)}, f32[2,2,4,16,256]{4,3,2,1,0:T(8,128)S(1)}, u32[]{:S(2)}) copy-start(f32[2,2,4,16,256]{4,3,2,1,0:T(8,128)S(1)} %collective-permute-done.1.refs_2_.refs_5_) | copy-start | bytes 786436
  26.2 13.1 %collective-permute-start.18 = (f32[4,2,8,128]{3,2,1,0:T(8,128)S(1)}, f32[4,2,8,128]{3,2,1,0:T(8,128)S(1)}, u32[]{:S(2)}, u32[]{:S(2)}) collective-permute-start(f32[4,2,8,128]{3,2,1,0:T(8,128)S(1)} %copy-done.26), channel_id=1, source_target_pairs={{1,16},{2,17},{3,18},{4,19},{5,20},{6,21},{7,22},{8,23},{9,24},{10... | collective-permute-start | bytes 98312 | tf_op jit(solution)/shard_map/ppermute | solution.py:343
  31.2 4.0 %copy-start.11 = (f32[2,2,4,16,256]{4,3,2,1,0:T(8,128)}, f32[2,2,4,16,256]{4,3,2,1,0:T(8,128)S(1)}, u32[]{:S(2)}) copy-start(f32[2,2,4,16,256]{4,3,2,1,0:T(8,128)S(1)} %collective-permute-done.22.refs_4_) | copy-start | bytes 786436
  31.2 8.1 %collective-permute-start.19 = (f32[4,2,8,128]{3,2,1,0:T(8,128)S(1)}, f32[4,2,8,128]{3,2,1,0:T(8,128)S(1)}, u32[]{:S(2)}, u32[]{:S(2)}) collective-permute-start(f32[4,2,8,128]{3,2,1,0:T(8,128)S(1)} %copy-done.26), channel_id=1, source_target_pairs={{2,16},{3,17},{4,18},{5,19},{6,20},{7,21},{8,22},{9,23},{10,24},{1... | collective-permute-start | bytes 98312 | tf_op jit(solution)/shard_map/ppermute | solution.py:343
  35.2 5.6 %copy-start.5 = (f32[1,2,4,16,256]{4,3,2,1,0:T(8,128)S(1)}, f32[1,2,4,16,256]{4,3,2,1,0:T(8,128)}, u32[]{:S(2)}) copy-start(f32[1,2,4,16,256]{4,3,2,1,0:T(8,128)} %fine.6.refs_3_) | copy-start | bytes 393220
  35.2 0.7 copy-start.12
  35.3 12.6 %collective-permute-start.2 = (f32[1,2,4,16,256]{4,3,2,1,0:T(8,128)}, f32[1,2,4,16,256]{4,3,2,1,0:T(8,128)S(1)}, u32[]{:S(2)}, u32[]{:S(2)}) collective-permute-start(f32[1,2,4,16,256]{4,3,2,1,0:T(8,128)} %fine.6.refs_3_), channel_id=1, source_target_pairs={{0,1},{1,0},{2,3},{3,2},{4,5},{5,4},{6,7},{7,6},{8,9},{9,8},{10,11... | collective-permute-start | bytes 393224 | tf_op jit(solution)/shard_map/ppermute | solution.py:333
  39.3 8.5 %copy-start.25 = (f32[4,2,8,128]{3,2,1,0:T(8,128)}, f32[4,2,8,128]{3,2,1,0:T(8,128)S(1)}, u32[]{:S(2)}) copy-start(f32[4,2,8,128]{3,2,1,0:T(8,128)S(1)} %collective-permute-done.18.refs_14_) | copy-start | bytes 98308
  39.3 32.3 %collective-permute-start.24 = (f32[2,2,4,16,256]{4,3,2,1,0:T(8,128)}, f32[2,2,4,16,256]{4,3,2,1,0:T(8,128)S(1)}, u32[]{:S(2)}, u32[]{:S(2)}) collective-permute-start(f32[2,2,4,16,256]{4,3,2,1,0:T(8,128)} %fine.8.refs_3_), channel_id=1, source_target_pairs={{0,1},{1,0},{2,3},{3,2},{4,5},{5,4},{6,7},{7,6},{8,9},{9,8},{10,11... | collective-permute-start | bytes 786440 | tf_op jit(solution)/shard_map/ppermute | solution.py:333
  39.3 8.4 %copy-start.27 = (f32[4,2,8,128]{3,2,1,0:T(8,128)}, f32[4,2,8,128]{3,2,1,0:T(8,128)S(1)}, u32[]{:S(2)}) copy-start(f32[4,2,8,128]{3,2,1,0:T(8,128)S(1)} %collective-permute-done.19.refs_15_) | copy-start | bytes 98308
  39.3 37.8 %collective-permute-start.25 = (f32[2,2,4,16,256]{4,3,2,1,0:T(8,128)}, f32[2,2,4,16,256]{4,3,2,1,0:T(8,128)S(1)}, u32[]{:S(2)}, u32[]{:S(2)}) collective-permute-start(f32[2,2,4,16,256]{4,3,2,1,0:T(8,128)} %fine.8.refs_3_), channel_id=1, source_target_pairs={{0,15},{1,2},{2,1},{3,4},{4,3},{5,6},{6,5},{7,8},{8,7},{9,10},{10,... | collective-permute-start | bytes 786440 | tf_op jit(solution)/shard_map/ppermute | solution.py:332
  40.8 4.3 %copy-start.13 = (f32[1,2,4,16,256]{4,3,2,1,0:T(8,128)}, f32[1,2,4,16,256]{4,3,2,1,0:T(8,128)S(1)}, u32[]{:S(2)}) copy-start(f32[1,2,4,16,256]{4,3,2,1,0:T(8,128)S(1)} %collective-permute-done.27.refs_4_) | copy-start | bytes 393220
  40.8 9.0 %collective-permute-start.3 = (f32[1,2,4,16,256]{4,3,2,1,0:T(8,128)S(1)}, f32[1,2,4,16,256]{4,3,2,1,0:T(8,128)S(1)}, u32[]{:S(2)}, u32[]{:S(2)}) collective-permute-start(f32[1,2,4,16,256]{4,3,2,1,0:T(8,128)S(1)} %copy-done.5), channel_id=1, source_target_pairs={{0,15},{1,2},{2,1},{3,4},{4,3},{5,6},{6,5},{7,8},{8,7},{9,10},{10,... | collective-permute-start | bytes 393224 | tf_op jit(solution)/shard_map/ppermute | solution.py:332
  43.9 1.3 %copy-start.15 = (f32[1,2,4,16,256]{4,3,2,1,0:T(8,128)}, f32[1,2,4,16,256]{4,3,2,1,0:T(8,128)S(1)}, u32[]{:S(2)}) copy-start(f32[1,2,4,16,256]{4,3,2,1,0:T(8,128)S(1)} %collective-permute-done.28.refs_5_) | copy-start | bytes 393220
  43.9 3.9 %collective-permute-start.20 = (f32[4,2,8,128]{3,2,1,0:T(8,128)S(1)}, f32[4,2,8,128]{3,2,1,0:T(8,128)S(1)}, u32[]{:S(2)}, u32[]{:S(2)}) collective-permute-start(f32[4,2,8,128]{3,2,1,0:T(8,128)S(1)} %copy-done.26), channel_id=1, source_target_pairs={{3,16},{4,17},{5,18},{6,19},{7,20},{8,21},{9,22},{10,23},{11,24},{... | collective-permute-start | bytes 98312 | tf_op jit(solution)/shard_map/ppermute | solution.py:343
  47.7 9.1 %copy-start.28 = (f32[4,2,8,128]{3,2,1,0:T(8,128)}, f32[4,2,8,128]{3,2,1,0:T(8,128)S(1)}, u32[]{:S(2)}) copy-start(f32[4,2,8,128]{3,2,1,0:T(8,128)S(1)} %collective-permute-done.20.refs_16_) | copy-start | bytes 98308
  47.7 15.9 %collective-permute-start.29 = (f32[1,2,4,16,256]{4,3,2,1,0:T(8,128)}, f32[1,2,4,16,256]{4,3,2,1,0:T(8,128)S(1)}, u32[]{:S(2)}, u32[]{:S(2)}) collective-permute-start(f32[1,2,4,16,256]{4,3,2,1,0:T(8,128)} %fine.10.refs_3_), channel_id=1, source_target_pairs={{0,1},{1,0},{2,3},{3,2},{4,5},{5,4},{6,7},{7,6},{8,9},{9,8},{10,11... | collective-permute-start | bytes 393224 | tf_op jit(solution)/shard_map/ppermute | solution.py:333
  47.8 6.2 %copy-start.17 = (f32[1,2,4,16,256]{4,3,2,1,0:T(8,128)}, f32[1,2,4,16,256]{4,3,2,1,0:T(8,128)S(1)}, u32[]{:S(2)}) copy-start(f32[1,2,4,16,256]{4,3,2,1,0:T(8,128)S(1)} %collective-permute-done.2.refs_4_) | copy-start | bytes 393220
  47.8 17.1 %collective-permute-start.30 = (f32[1,2,4,16,256]{4,3,2,1,0:T(8,128)}, f32[1,2,4,16,256]{4,3,2,1,0:T(8,128)S(1)}, u32[]{:S(2)}, u32[]{:S(2)}) collective-permute-start(f32[1,2,4,16,256]{4,3,2,1,0:T(8,128)} %fine.10.refs_3_), channel_id=1, source_target_pairs={{0,15},{1,2},{2,1},{3,4},{4,3},{5,6},{6,5},{7,8},{8,7},{9,10},{10,... | collective-permute-start | bytes 393224 | tf_op jit(solution)/shard_map/ppermute | solution.py:332
  49.8 4.2 %copy-start.18 = (f32[1,2,4,16,256]{4,3,2,1,0:T(8,128)}, f32[1,2,4,16,256]{4,3,2,1,0:T(8,128)S(1)}, u32[]{:S(2)}) copy-start(f32[1,2,4,16,256]{4,3,2,1,0:T(8,128)S(1)} %collective-permute-done.3.refs_5_) | copy-start | bytes 393220
  49.8 7.0 %collective-permute-start.21 = (f32[4,2,8,128]{3,2,1,0:T(8,128)S(1)}, f32[4,2,8,128]{3,2,1,0:T(8,128)S(1)}, u32[]{:S(2)}, u32[]{:S(2)}) collective-permute-start(f32[4,2,8,128]{3,2,1,0:T(8,128)S(1)} %copy-done.26), channel_id=1, source_target_pairs={{4,16},{5,17},{6,18},{7,19},{8,20},{9,21},{10,22},{11,23},{12,24},... | collective-permute-start | bytes 98312 | tf_op jit(solution)/shard_map/ppermute | solution.py:343
  56.8 25.4 %copy-start.29 = (f32[4,2,8,128]{3,2,1,0:T(8,128)}, f32[4,2,8,128]{3,2,1,0:T(8,128)S(1)}, u32[]{:S(2)}) copy-start(f32[4,2,8,128]{3,2,1,0:T(8,128)S(1)} %collective-permute-done.21.refs_17_) | copy-start | bytes 98308
  56.8 9.5 %collective-permute-start.10 = (f32[2,2,8,128]{3,2,1,0:T(8,128)}, f32[2,2,8,128]{3,2,1,0:T(8,128)S(1)}, u32[]{:S(2)}, u32[]{:S(2)}) collective-permute-start(f32[2,2,8,128]{3,2,1,0:T(8,128)} %get-tuple-element.7), channel_id=1, source_target_pairs={{2,16},{3,17},{4,18},{5,19},{6,20},{7,21},{8,22},{9,23},{10,24},{1... | collective-permute-start | bytes 49160 | tf_op jit(solution)/shard_map/ppermute | solution.py:343
  63.7 16.0 %copy-start.14 = (f32[1,2,4,16,256]{4,3,2,1,0:T(8,128)}, f32[1,2,4,16,256]{4,3,2,1,0:T(8,128)S(1)}, u32[]{:S(2)}) copy-start(f32[1,2,4,16,256]{4,3,2,1,0:T(8,128)S(1)} %collective-permute-done.29.refs_4_) | copy-start | bytes 393220
  63.7 3.9 %collective-permute-start.11 = (f32[2,2,8,128]{3,2,1,0:T(8,128)}, f32[2,2,8,128]{3,2,1,0:T(8,128)S(1)}, u32[]{:S(2)}, u32[]{:S(2)}) collective-permute-start(f32[2,2,8,128]{3,2,1,0:T(8,128)} %get-tuple-element.7), channel_id=1, source_target_pairs={{3,16},{4,17},{5,18},{6,19},{7,20},{8,21},{9,22},{10,23},{11,24},{... | collective-permute-start | bytes 49160 | tf_op jit(solution)/shard_map/ppermute | solution.py:343
  65.0 14.7 %copy-start.16 = (f32[1,2,4,16,256]{4,3,2,1,0:T(8,128)}, f32[1,2,4,16,256]{4,3,2,1,0:T(8,128)S(1)}, u32[]{:S(2)}) copy-start(f32[1,2,4,16,256]{4,3,2,1,0:T(8,128)S(1)} %collective-permute-done.30.refs_5_) | copy-start | bytes 393220
  65.0 3.9 %collective-permute-start.12 = (f32[2,2,8,128]{3,2,1,0:T(8,128)}, f32[2,2,8,128]{3,2,1,0:T(8,128)S(1)}, u32[]{:S(2)}, u32[]{:S(2)}) collective-permute-start(f32[2,2,8,128]{3,2,1,0:T(8,128)} %get-tuple-element.7), channel_id=1, source_target_pairs={{4,16},{5,17},{6,18},{7,19},{8,20},{9,21},{10,22},{11,23},{12,24},... | collective-permute-start | bytes 49160 | tf_op jit(solution)/shard_map/ppermute | solution.py:343
  66.3 15.9 %copy-start.30 = (f32[2,2,8,128]{3,2,1,0:T(8,128)}, f32[2,2,8,128]{3,2,1,0:T(8,128)S(1)}, u32[]{:S(2)}) copy-start(f32[2,2,8,128]{3,2,1,0:T(8,128)S(1)} %collective-permute-done.10.refs_6_) | copy-start | bytes 49156
  66.3 3.9 %collective-permute-start.4 = (f32[2,2,8,128]{3,2,1,0:T(8,128)}, f32[2,2,8,128]{3,2,1,0:T(8,128)S(1)}, u32[]{:S(2)}, u32[]{:S(2)}) collective-permute-start(f32[2,2,8,128]{3,2,1,0:T(8,128)} %get-tuple-element.7), channel_id=1, source_target_pairs={{12,16},{13,17},{14,18},{15,19},{0,20},{1,21},{2,22},{3,23},{4,24}... | collective-permute-start | bytes 49160 | tf_op jit(solution)/shard_map/ppermute | solution.py:343
  67.6 14.6 %copy-start.31 = (f32[2,2,8,128]{3,2,1,0:T(8,128)}, f32[2,2,8,128]{3,2,1,0:T(8,128)S(1)}, u32[]{:S(2)}) copy-start(f32[2,2,8,128]{3,2,1,0:T(8,128)S(1)} %collective-permute-done.11.refs_7_) | copy-start | bytes 49156
  67.6 17.9 %collective-permute-start.5 = (f32[2,2,8,128]{3,2,1,0:T(8,128)}, f32[2,2,8,128]{3,2,1,0:T(8,128)S(1)}, u32[]{:S(2)}, u32[]{:S(2)}) collective-permute-start(f32[2,2,8,128]{3,2,1,0:T(8,128)} %get-tuple-element.7), channel_id=1, source_target_pairs={{13,16},{14,17},{15,18},{0,19},{1,20},{2,21},{3,22},{4,23},{5,24},... | collective-permute-start | bytes 49160 | tf_op jit(solution)/shard_map/ppermute | solution.py:343
  68.9 13.2 %copy-start.32 = (f32[2,2,8,128]{3,2,1,0:T(8,128)}, f32[2,2,8,128]{3,2,1,0:T(8,128)S(1)}, u32[]{:S(2)}) copy-start(f32[2,2,8,128]{3,2,1,0:T(8,128)S(1)} %collective-permute-done.12.refs_8_) | copy-start | bytes 49156
  68.9 16.6 %collective-permute-start.6 = (f32[2,2,8,128]{3,2,1,0:T(8,128)}, f32[2,2,8,128]{3,2,1,0:T(8,128)S(1)}, u32[]{:S(2)}, u32[]{:S(2)}) collective-permute-start(f32[2,2,8,128]{3,2,1,0:T(8,128)} %get-tuple-element.7), channel_id=1, source_target_pairs={{14,16},{15,17},{0,18},{1,19},{2,20},{3,21},{4,22},{5,23},{6,24},{... | collective-permute-start | bytes 49160 | tf_op jit(solution)/shard_map/ppermute | solution.py:343
  70.3 11.9 %copy-start.33 = (f32[2,2,8,128]{3,2,1,0:T(8,128)}, f32[2,2,8,128]{3,2,1,0:T(8,128)S(1)}, u32[]{:S(2)}) copy-start(f32[2,2,8,128]{3,2,1,0:T(8,128)S(1)} %collective-permute-done.4.refs_0_) | copy-start | bytes 49156
  70.3 15.3 %collective-permute-start.7 = (f32[2,2,8,128]{3,2,1,0:T(8,128)}, f32[2,2,8,128]{3,2,1,0:T(8,128)S(1)}, u32[]{:S(2)}, u32[]{:S(2)}) collective-permute-start(f32[2,2,8,128]{3,2,1,0:T(8,128)} %get-tuple-element.7), channel_id=1, source_target_pairs={{15,16},{0,17},{1,18},{2,19},{3,20},{4,21},{5,22},{6,23},{7,24},{8... | collective-permute-start | bytes 49160 | tf_op jit(solution)/shard_map/ppermute | solution.py:343
  71.6 10.6 %copy-start.9 = (f32[2,2,4,16,256]{4,3,2,1,0:T(8,128)}, f32[2,2,4,16,256]{4,3,2,1,0:T(8,128)S(1)}, u32[]{:S(2)}) copy-start(f32[2,2,4,16,256]{4,3,2,1,0:T(8,128)S(1)} %collective-permute-done.24.refs_4_) | copy-start | bytes 786436
  71.6 14.0 %collective-permute-start.8 = (f32[2,2,8,128]{3,2,1,0:T(8,128)}, f32[2,2,8,128]{3,2,1,0:T(8,128)S(1)}, u32[]{:S(2)}, u32[]{:S(2)}) collective-permute-start(f32[2,2,8,128]{3,2,1,0:T(8,128)} %get-tuple-element.7), channel_id=1, source_target_pairs={{0,16},{1,17},{2,18},{3,19},{4,20},{5,21},{6,22},{7,23},{8,24},{9,... | collective-permute-start | bytes 49160 | tf_op jit(solution)/shard_map/ppermute | solution.py:343
  77.2 5.1 %copy-start.10 = (f32[2,2,4,16,256]{4,3,2,1,0:T(8,128)}, f32[2,2,4,16,256]{4,3,2,1,0:T(8,128)S(1)}, u32[]{:S(2)}) copy-start(f32[2,2,4,16,256]{4,3,2,1,0:T(8,128)S(1)} %collective-permute-done.25.refs_5_) | copy-start | bytes 786436
  77.2 8.4 %collective-permute-start.9 = (f32[2,2,8,128]{3,2,1,0:T(8,128)}, f32[2,2,8,128]{3,2,1,0:T(8,128)S(1)}, u32[]{:S(2)}, u32[]{:S(2)}) collective-permute-start(f32[2,2,8,128]{3,2,1,0:T(8,128)} %get-tuple-element.7), channel_id=1, source_target_pairs={{1,16},{2,17},{3,18},{4,19},{5,20},{6,21},{7,22},{8,23},{9,24},{10... | collective-permute-start | bytes 49160 | tf_op jit(solution)/shard_map/ppermute | solution.py:343
  (6 other events, 3.7 us)
